TPU v7x, 256 devices: a whole 4x4x8 slice. The times are simulated.
256 devices in a mesh: gx: 32 (over z, x_lo, core), gy: 8 (over x_hi, y).
Axes of the slice: x: 4 (x_hi: 2, x_lo: 2; x = x_hi * 2 + x_lo), y: 4, z: 8, core: 2. Of those that a mesh axis runs over, the one named last changes fastest.
Arguments:
- volt: float32 [256, 512, 2048], P('gx', 'gy'), may hold values from -6 to 6
- drive: float32 [256, 512, 2048], P('gx', 'gy'), may hold values from -6 to 6
- region: int32 [256, 512, 32], P('gx', 'gy'), may hold values from 0 to 7
- diode_mask: int32 [256, 512, 32], P('gx', 'gy'), may hold values 0 or 1
- sigma_table: float32 [8], replicated, may hold values from 0.3 to 3
- cap_table: float32 [8], replicated, may hold values from 0.1 to 1
Outputs:
- residual: float32 [256, 512, 2048], P('gx', 'gy')
- coef_norms: float32 [64], replicated
All inputs are finite; a program needn't handle non-finite values. No bound on the sum of `diode_mask` on one device may be relied on, other than what follows from the above.
Results may differ from a plain program's by a relative error of at most 0.0003.
Values sent between devices are 32-bit elements; how exact they have to be, the bound alone decides.
A program may use at most 192 MiB of HBM per device.

v0:
```python
import functools
import math

import jax
import jax.numpy as jnp
from jax import lax
from jax.sharding import Mesh
from jax.sharding import PartitionSpec as P

NZ = 32
H = 32
KC = 64
S = 256
GX = ("gx_0", "gx_1", "gx_2")
GY = ("gy_0", "gy_1")
GX_GY = ("gx_0", "gx_1", "gx_2", "gy_0", "gy_1")


base_freq = 0.1
norm_eps = 1e-06


def padded_2(block, sides, width, periodic):
    for axis, dim in sides:
        count = lax.axis_size(axis)
        forward = [(i, i + 1) for i in range(count - 1)]
        if periodic:
            forward.append((count - 1, 0))
        backward = [(target, source) for source, target in forward]
        low = lax.ppermute(
            lax.slice_in_dim(block, block.shape[dim] - width, None, axis=dim), axis, forward
        )
        high = lax.ppermute(lax.slice_in_dim(block, 0, width, axis=dim), axis, backward)
        block = jnp.concatenate([low, block, high], axis=dim)
    return block


def over_axes(array, axes):
    return functools.reduce(lax.psum, axes, array)


def cut_slab(array, first_idx, last_idx, along):
    return lax.slice_in_dim(array, first_idx, last_idx, axis=along)


def harmonic_mean(left, right):
    return 2.0 * left * right / (left + right)


def open_terms(volt_field, conduct, along):
    cell_count = volt_field.shape[along]
    widths = [(0, 0)] * volt_field.ndim
    widths[along] = (1, 1)
    padded_volt = jnp.pad(volt_field, widths)
    padded_cond = jnp.pad(conduct, widths)
    face_flux = harmonic_mean(
        cut_slab(padded_cond, 0, cell_count + 1, along),
        cut_slab(padded_cond, 1, cell_count + 2, along),
    ) * (
        cut_slab(padded_volt, 1, cell_count + 2, along)
        - cut_slab(padded_volt, 0, cell_count + 1, along)
    )
    return cut_slab(face_flux, 0, cell_count, along) - cut_slab(face_flux, 1, cell_count + 1, along)


def time_derivative(coefs):
    half_count = coefs.shape[-1] // 2
    orders = base_freq * jnp.arange(1, half_count + 1, dtype=jnp.float32)
    return jnp.concatenate(
        [orders * coefs[..., half_count:], -orders * coefs[..., :half_count]], axis=-1
    )


def spectral_tables(harmonics, samples):
    orders = jnp.arange(1, harmonics + 1, dtype=jnp.float32)
    times = 2.0 * math.pi * jnp.arange(samples, dtype=jnp.float32) / samples
    angles = orders[:, None] * times[None, :]
    synthesis = jnp.concatenate([jnp.cos(angles), jnp.sin(angles)], axis=0)
    analysis = synthesis.T * (2.0 / samples)
    return (synthesis, analysis)


def nonlinear_row(volt_row, diode_row, synthesis, analysis):
    coef_count = volt_row.shape[-1]
    flat = volt_row.reshape(-1, coef_count)
    cell_count = flat.shape[0]
    samples = jnp.dot(
        flat, synthesis, precision=lax.Precision.HIGHEST, preferred_element_type=jnp.float32
    )
    current = jax.nn.softplus(2.0 * samples) * 0.5
    charge = jnp.tanh(samples) * 0.5
    projected = jnp.dot(
        jnp.concatenate([current, charge], axis=0),
        analysis,
        precision=lax.Precision.HIGHEST,
        preferred_element_type=jnp.float32,
    )
    combined = projected[:cell_count] + time_derivative(projected[cell_count:])
    return combined.reshape(volt_row.shape) * diode_row[..., None]


def lookup(region, region_table):
    onehot = (region[..., None] == jnp.arange(region_table.shape[0], dtype=jnp.int32)).astype(
        jnp.float32
    )
    return jnp.sum(onehot * region_table, axis=-1)


def unpack(packed_block):
    row_width = NZ * KC
    volt_part = packed_block[..., :row_width].reshape(packed_block.shape[:-1] + (NZ, KC))
    cond_part = packed_block[..., row_width : row_width + NZ][..., None]
    return (volt_part, cond_part)


def edge_flux(low_block, high_block):
    low_volt, low_cond = unpack(low_block)
    high_volt, high_cond = unpack(high_block)
    return harmonic_mean(low_cond, high_cond) * (high_volt - low_volt)


def face_terms_both(padded, along, cell_count):
    face_flux = edge_flux(
        cut_slab(padded, 0, cell_count + 1, along), cut_slab(padded, 1, cell_count + 2, along)
    )
    return cut_slab(face_flux, 0, cell_count, along) - cut_slab(face_flux, 1, cell_count + 1, along)


def body(volt, drive, region, diode_mask, sigma_table, cap_table):
    rows_local, cols_local, row_width = volt.shape
    conduct = lookup(region, sigma_table)
    capacity = lookup(region, cap_table)[..., None]
    padding = jnp.zeros((rows_local, cols_local, 128 - NZ), jnp.float32)
    packed = jnp.concatenate([volt, conduct, padding], axis=2)
    volt_field = volt.reshape(rows_local, cols_local, NZ, KC)
    padded_rows = padded_2(packed, ((GX, 0),), 1, True)
    row_terms = face_terms_both(padded_rows, 0, rows_local)
    padded_cols = padded_2(packed, ((GY, 1),), 1, False)
    col_terms = face_terms_both(padded_cols, 1, cols_local)
    depth_terms = open_terms(volt_field, conduct[..., None], 2)
    synthesis, analysis = spectral_tables(H, S)
    diode_field = diode_mask.astype(jnp.float32)

    def diode_rows(pair):
        return nonlinear_row(pair[0], pair[1], synthesis, analysis)

    diode_part = lax.map(diode_rows, (volt_field, diode_field))
    drive_field = drive.reshape(rows_local, cols_local, NZ, KC)
    residual = (
        row_terms
        + col_terms
        + depth_terms
        + capacity * time_derivative(volt_field)
        + diode_part
        - drive_field
    )
    partial_value = jnp.sum(residual * residual, axis=(0, 1, 2))
    summed = over_axes(partial_value, GX_GY)
    cells_total = rows_local * cols_local * NZ * lax.axis_size(GX) * lax.axis_size(GY)
    norms_out = jnp.sqrt(summed / cells_total + norm_eps)
    return (residual.reshape(rows_local, cols_local, row_width), norms_out)


def solution(mesh):
    finer = Mesh(mesh.devices.reshape(8, 2, 2, 2, 4), ("gx_0", "gx_1", "gx_2", "gy_0", "gy_1"))
    in_specs = (P(GX, GY, None), P(GX, GY, None), P(GX, GY, None), P(GX, GY, None), P(), P())
    out_specs = (P(GX, GY, None), P())
    return jax.shard_map(body, mesh=finer, in_specs=in_specs, out_specs=out_specs, check_vma=False)
```

profile of v0, /device:TPU:1, one launch (start us, length us, event | category | flops | bytes accessed | tf_op | source)
XLA Modules:
  0.0 278.5 jit_solution(14886055668205441552)
XLA Ops:
  0.6 1.6 select_reduce_fusion
  2.4 5.9 %concatenate.29 = f32[8,64,2176]{2,1,0:T(8,128)} concatenate(f32[8,64,2048]{2,1,0:T(8,128)} %param.8, f32[8,64,32]{2,1,0:T(8,128)S(1)} %copy.52, f32[8,64,96]{2,1,0:T(8,128)S(1)} %broadcast_in_dim.7), dimensions={2} | concatenate | bytes 8912896 | tf_op jit(solution)/shard_map/concatenate | solution.py:134
  8.3 2.3 fusion.18
  10.7 2.6 collective-permute-start
  13.3 0.6 collective-permute-start.1
  13.9 1.3 fusion.19
  15.2 2.6 collective-permute-start.2
  17.8 1.5 collective-permute-start.3
  19.3 7.8 %reshape.76 = f32[8,64,32,64]{3,2,1,0:T(8,128)} reshape(f32[8,64,2048]{2,1,0:T(8,128)} %param.8) | data formatting | bytes 8388608 | tf_op jit(solution)/shard_map/reshape | solution.py:135
  27.2 0.5 broadcast_multiply_fusion.2
  27.9 0.6 multiply_bitcast_fusion
  28.8 90.9 %while.10 = (s32[]{:T(128)}, f32[8,64,32,64]{3,2,1,0:T(8,128)}, f32[8,64,32,64]{3,2,1,0:T(8,128)}, f32[64,256]{1,0:T(8,128)}, f32[256,64]{1,0:T(8,128)S(1)}, /*index=5*/f32[8,64,32]{2,1,0:T(8,128)S(1)}, s32[]{:T(128)}) while((s32[]{:T(128)}, f32[8,64,32,64]{3,2,1,0:T(8,128)}, f32[8,64,32,64]{3,2,1,0:T(8,128)}, f32[64,256]{1,0:T(8,128)}, ...), condition=%wide.region_3.4_spmd, body=%wide.region_2.3_spmd.sunk | while | flops 1214251136 | bytes 16409685 | solution.py:147
  28.8 1.3 constant_dynamic-slice_fusion.2
  30.1 3.9 %fusion.33 = (f32[2048,256]{1,0:T(8,128)S(1)}, f32[2048,256]{1,0:T(8,128)S(1)}) fusion(f32[2048,64]{1,0:T(8,128)S(1)} %bitcast.31, f32[64,256]{1,0:T(8,128)} %get-tuple-element.147), kind=kOutput, calls=%fused_computation.5.clone.1 | convolution fusion | flops 407371776 | bytes 4784128 | tf_op jit(solution)/shard_map/while/body/eval_jaxpr/dot_general | solution.py:87
  34.0 4.2 %fusion.34 = f32[4096,64]{0,1:T(8,128)S(1)} fusion(f32[256,64]{1,0:T(8,128)S(1)} %get-tuple-element.148, f32[2048,256]{1,0:T(8,128)S(1)} %get-tuple-element.124, f32[2048,256]{1,0:T(8,128)S(1)} %get-tuple-element.125), kind=kOutput, calls=%fused_computation.1.clone.1 | convolution fusion | flops 806354944 | bytes 5308416 | tf_op jit(solution)/shard_map/while/body/eval_jaxpr/dot_general | solution.py:92
  38.5 0.3 copy.65
  38.8 1.4 multiply_dynamic-update-slice_fusion.2
  40.2 1.3 constant_dynamic-slice_fusion.2
  41.5 3.9 %fusion.33 = (f32[2048,256]{1,0:T(8,128)S(1)}, f32[2048,256]{1,0:T(8,128)S(1)}) fusion(f32[2048,64]{1,0:T(8,128)S(1)} %bitcast.31, f32[64,256]{1,0:T(8,128)} %get-tuple-element.147), kind=kOutput, calls=%fused_computation.5.clone.1 | convolution fusion | flops 407371776 | bytes 4784128 | tf_op jit(solution)/shard_map/while/body/eval_jaxpr/dot_general | solution.py:87
  45.4 4.2 %fusion.34 = f32[4096,64]{0,1:T(8,128)S(1)} fusion(f32[256,64]{1,0:T(8,128)S(1)} %get-tuple-element.148, f32[2048,256]{1,0:T(8,128)S(1)} %get-tuple-element.124, f32[2048,256]{1,0:T(8,128)S(1)} %get-tuple-element.125), kind=kOutput, calls=%fused_computation.1.clone.1 | convolution fusion | flops 806354944 | bytes 5308416 | tf_op jit(solution)/shard_map/while/body/eval_jaxpr/dot_general | solution.py:92
  50.2 1.3 multiply_dynamic-update-slice_fusion.2
  51.6 1.3 constant_dynamic-slice_fusion.2
  52.9 3.9 %fusion.33 = (f32[2048,256]{1,0:T(8,128)S(1)}, f32[2048,256]{1,0:T(8,128)S(1)}) fusion(f32[2048,64]{1,0:T(8,128)S(1)} %bitcast.31, f32[64,256]{1,0:T(8,128)} %get-tuple-element.147), kind=kOutput, calls=%fused_computation.5.clone.1 | convolution fusion | flops 407371776 | bytes 4784128 | tf_op jit(solution)/shard_map/while/body/eval_jaxpr/dot_general | solution.py:87
  56.8 4.2 %fusion.34 = f32[4096,64]{0,1:T(8,128)S(1)} fusion(f32[256,64]{1,0:T(8,128)S(1)} %get-tuple-element.148, f32[2048,256]{1,0:T(8,128)S(1)} %get-tuple-element.124, f32[2048,256]{1,0:T(8,128)S(1)} %get-tuple-element.125), kind=kOutput, calls=%fused_computation.1.clone.1 | convolution fusion | flops 806354944 | bytes 5308416 | tf_op jit(solution)/shard_map/while/body/eval_jaxpr/dot_general | solution.py:92
  61.6 1.3 multiply_dynamic-update-slice_fusion.2
  62.9 1.3 constant_dynamic-slice_fusion.2
  64.2 3.9 %fusion.33 = (f32[2048,256]{1,0:T(8,128)S(1)}, f32[2048,256]{1,0:T(8,128)S(1)}) fusion(f32[2048,64]{1,0:T(8,128)S(1)} %bitcast.31, f32[64,256]{1,0:T(8,128)} %get-tuple-element.147), kind=kOutput, calls=%fused_computation.5.clone.1 | convolution fusion | flops 407371776 | bytes 4784128 | tf_op jit(solution)/shard_map/while/body/eval_jaxpr/dot_general | solution.py:87
  68.1 4.2 %fusion.34 = f32[4096,64]{0,1:T(8,128)S(1)} fusion(f32[256,64]{1,0:T(8,128)S(1)} %get-tuple-element.148, f32[2048,256]{1,0:T(8,128)S(1)} %get-tuple-element.124, f32[2048,256]{1,0:T(8,128)S(1)} %get-tuple-element.125), kind=kOutput, calls=%fused_computation.1.clone.1 | convolution fusion | flops 806354944 | bytes 5308416 | tf_op jit(solution)/shard_map/while/body/eval_jaxpr/dot_general | solution.py:92
  72.9 1.3 multiply_dynamic-update-slice_fusion.2
  74.2 1.3 constant_dynamic-slice_fusion.2
  75.5 3.9 %fusion.33 = (f32[2048,256]{1,0:T(8,128)S(1)}, f32[2048,256]{1,0:T(8,128)S(1)}) fusion(f32[2048,64]{1,0:T(8,128)S(1)} %bitcast.31, f32[64,256]{1,0:T(8,128)} %get-tuple-element.147), kind=kOutput, calls=%fused_computation.5.clone.1 | convolution fusion | flops 407371776 | bytes 4784128 | tf_op jit(solution)/shard_map/while/body/eval_jaxpr/dot_general | solution.py:87
  79.5 4.2 %fusion.34 = f32[4096,64]{0,1:T(8,128)S(1)} fusion(f32[256,64]{1,0:T(8,128)S(1)} %get-tuple-element.148, f32[2048,256]{1,0:T(8,128)S(1)} %get-tuple-element.124, f32[2048,256]{1,0:T(8,128)S(1)} %get-tuple-element.125), kind=kOutput, calls=%fused_computation.1.clone.1 | convolution fusion | flops 806354944 | bytes 5308416 | tf_op jit(solution)/shard_map/while/body/eval_jaxpr/dot_general | solution.py:92
  84.3 1.3 multiply_dynamic-update-slice_fusion.2
  85.6 1.3 constant_dynamic-slice_fusion.2
  86.9 3.9 %fusion.33 = (f32[2048,256]{1,0:T(8,128)S(1)}, f32[2048,256]{1,0:T(8,128)S(1)}) fusion(f32[2048,64]{1,0:T(8,128)S(1)} %bitcast.31, f32[64,256]{1,0:T(8,128)} %get-tuple-element.147), kind=kOutput, calls=%fused_computation.5.clone.1 | convolution fusion | flops 407371776 | bytes 4784128 | tf_op jit(solution)/shard_map/while/body/eval_jaxpr/dot_general | solution.py:87
  90.8 4.2 %fusion.34 = f32[4096,64]{0,1:T(8,128)S(1)} fusion(f32[256,64]{1,0:T(8,128)S(1)} %get-tuple-element.148, f32[2048,256]{1,0:T(8,128)S(1)} %get-tuple-element.124, f32[2048,256]{1,0:T(8,128)S(1)} %get-tuple-element.125), kind=kOutput, calls=%fused_computation.1.clone.1 | convolution fusion | flops 806354944 | bytes 5308416 | tf_op jit(solution)/shard_map/while/body/eval_jaxpr/dot_general | solution.py:92
  95.6 1.3 multiply_dynamic-update-slice_fusion.2
  96.9 1.3 constant_dynamic-slice_fusion.2
  98.2 3.9 %fusion.33 = (f32[2048,256]{1,0:T(8,128)S(1)}, f32[2048,256]{1,0:T(8,128)S(1)}) fusion(f32[2048,64]{1,0:T(8,128)S(1)} %bitcast.31, f32[64,256]{1,0:T(8,128)} %get-tuple-element.147), kind=kOutput, calls=%fused_computation.5.clone.1 | convolution fusion | flops 407371776 | bytes 4784128 | tf_op jit(solution)/shard_map/while/body/eval_jaxpr/dot_general | solution.py:87
  102.2 4.2 %fusion.34 = f32[4096,64]{0,1:T(8,128)S(1)} fusion(f32[256,64]{1,0:T(8,128)S(1)} %get-tuple-element.148, f32[2048,256]{1,0:T(8,128)S(1)} %get-tuple-element.124, f32[2048,256]{1,0:T(8,128)S(1)} %get-tuple-element.125), kind=kOutput, calls=%fused_computation.1.clone.1 | convolution fusion | flops 806354944 | bytes 5308416 | tf_op jit(solution)/shard_map/while/body/eval_jaxpr/dot_general | solution.py:92
  107.0 1.4 multiply_dynamic-update-slice_fusion.2
  108.3 1.3 constant_dynamic-slice_fusion.2
  109.6 3.9 %fusion.33 = (f32[2048,256]{1,0:T(8,128)S(1)}, f32[2048,256]{1,0:T(8,128)S(1)}) fusion(f32[2048,64]{1,0:T(8,128)S(1)} %bitcast.31, f32[64,256]{1,0:T(8,128)} %get-tuple-element.147), kind=kOutput, calls=%fused_computation.5.clone.1 | convolution fusion | flops 407371776 | bytes 4784128 | tf_op jit(solution)/shard_map/while/body/eval_jaxpr/dot_general | solution.py:87
  113.5 4.2 %fusion.34 = f32[4096,64]{0,1:T(8,128)S(1)} fusion(f32[256,64]{1,0:T(8,128)S(1)} %get-tuple-element.148, f32[2048,256]{1,0:T(8,128)S(1)} %get-tuple-element.124, f32[2048,256]{1,0:T(8,128)S(1)} %get-tuple-element.125), kind=kOutput, calls=%fused_computation.1.clone.1 | convolution fusion | flops 806354944 | bytes 5308416 | tf_op jit(solution)/shard_map/while/body/eval_jaxpr/dot_general | solution.py:92
  118.3 1.3 multiply_dynamic-update-slice_fusion.2
  119.9 13.0 %slice_multiply_fusion.3 = (f32[8,64,32,32]{3,2,1,0:T(8,128)}, f32[8,64,32,32]{3,2,1,0:T(8,128)}) fusion(f32[8,64,32,64]{3,2,1,0:T(8,128)} %get-tuple-element.151, f32[32]{0:T(128)S(1)} %get-tuple-element.79, f32[32]{0:T(128)} %get-tuple-element.80), kind=kLoop, calls=%fused_computation.21 | loop fusion | flops 1048576 | bytes 8388864 | tf_op jit(solution)/shard_map/mul | solution.py:70
  132.9 6.8 %fusion.8 = f32[8,64,33,64]{3,2,1,0:T(8,128)} fusion(f32[8,64,32,64]{3,2,1,0:T(8,128)S(1)} %copy-done, f32[8,64,33]{2,1,0:T(8,128)S(1)} %copy.59), kind=kLoop, calls=%fused_computation.19 | loop fusion | flops 2162688 | bytes 8587264 | tf_op jit(solution)/shard_map/mul | solution.py:56
  139.8 7.8 %reshape.77 = f32[8,64,32,64]{3,2,1,0:T(8,128)} reshape(f32[8,64,2048]{2,1,0:T(8,128)} %param.9) | data formatting | bytes 8388608 | tf_op jit(solution)/shard_map/reshape | solution.py:148
  147.7 1.1 copy.56
  148.8 7.3 %fusion.14 = f32[8,65,2048]{2,1,0:T(8,128)} fusion(f32[8,64,2176]{2,1,0:T(8,128)} %concatenate.29, f32[8,1,2176]{2,1,0:T(1,128)S(1)} %copy.54, f32[8,1,2176]{2,1,0:T(1,128)S(1)} %copy.56), kind=kLoop, calls=%fused_computation.33 | loop fusion | flops 3194880 | bytes 8855552 | tf_op jit(solution)/shard_map/sub | solution.py:119
  156.2 7.6 %reshape.79 = f32[8,65,32,64]{3,2,1,0:T(8,128)} reshape(f32[8,65,2048]{2,1,0:T(8,128)} %fusion.14) | data formatting | bytes 8519680 | tf_op jit(solution)/shard_map/sub | solution.py:119
  163.9 8.4 %broadcast_multiply_fusion.1 = f32[8,65,32,64]{3,2,1,0:T(8,128)} fusion(f32[8,65,32,64]{3,2,1,0:T(8,128)} %reshape.79, f32[8,65,32]{2,1,0:T(8,128)S(1)} %add_divide_fusion), kind=kLoop, calls=%fused_computation.39 | loop fusion | flops 1064960 | bytes 8586240 | tf_op jit(solution)/shard_map/mul | solution.py:119
  172.3 2.8 fusion.15
  175.1 8.7 %sub.28 = f32[9,64,32,64]{3,2,1,0:T(8,128)} reshape(f32[9,64,2048]{2,1,0:T(8,128)} %fusion.15) | data formatting | bytes 9437184 | tf_op jit(solution)/shard_map/sub | solution.py:119
  183.8 1.2 add_divide_fusion.1
  185.0 8.7 %broadcast_multiply_fusion = f32[9,64,32,64]{3,2,1,0:T(8,128)} fusion(f32[9,64,32,64]{3,2,1,0:T(8,128)} %sub.28, f32[9,64,32]{2,1,0:T(8,128)S(1)} %add_divide_fusion.1), kind=kLoop, calls=%fused_computation.38 | loop fusion | flops 1179648 | bytes 9510912 | tf_op jit(solution)/shard_map/mul | solution.py:119
  193.7 31.9 %multiply_reduce_fusion = (f32[64]{0:T(128)S(1)}, f32[8,64,32,64]{3,2,1,0:T(8,128)}) fusion(f32[8,64,32,64]{3,2,1,0:T(8,128)} %reshape.77, f32[8,64,32,64]{3,2,1,0:T(8,128)} %get-tuple-element.34, f32[8,64,32,32]{3,2,1,0:T(8,128)} %get-tuple-element.70, f32[8,64,32,32]{3,2,1,0:T(8,128)} %get-tuple-element.69, f32[8,64,32]{2,1,0:T(8,128)S(1)} %copy.60, ...), kind=kLoop, calls=%fused_computation.31 | loop fusion | flops 12582848 | bytes 42008832 | tf_op jit(solution)/shard_map/reduce_sum | solution.py:157
  225.6 7.8 %reshape.78 = f32[8,64,2048]{2,1,0:T(8,128)} reshape(f32[8,64,32,64]{3,2,1,0:T(8,128)} %get-tuple-element.62) | data formatting | bytes 8388608 | tf_op jit(solution)/shard_map/reshape | solution.py:161
  233.4 16.2 %psum.35 = f32[64]{0:T(128)S(1)} all-reduce(f32[64]{0:T(128)S(1)} %get-tuple-element.61), channel_id=1, replica_groups=mesh['gx_0'=8,'gx_1'=2,'gx_2'=2,'gy_0'=2,'gy_1'=4] {'gx_0'}, use_global_device_ids=true, to_apply=%region_5.6 | all-reduce | flops 64 | bytes 512 | tf_op jit(solution)/shard_map/psum | solution.py:39
  249.7 3.8 %psum.36 = f32[64]{0:T(128)S(1)} all-reduce(f32[64]{0:T(128)S(1)} %psum.35), channel_id=1, replica_groups=mesh['gx_0'=8,'gx_1'=2,'gx_2'=2,'gy_0'=2,'gy_1'=4] {'gx_1'}, use_global_device_ids=true, to_apply=%region_6.7 | all-reduce | flops 64 | bytes 512 | tf_op jit(solution)/shard_map/psum | solution.py:39
  253.4 8.8 %psum.37 = f32[64]{0:T(128)S(1)} all-reduce(f32[64]{0:T(128)S(1)} %psum.36), channel_id=1, replica_groups=mesh['gx_0'=8,'gx_1'=2,'gx_2'=2,'gy_0'=2,'gy_1'=4] {'gx_2'}, use_global_device_ids=true, to_apply=%region_7.8 | all-reduce | flops 64 | bytes 512 | tf_op jit(solution)/shard_map/psum | solution.py:39
  262.3 9.7 %psum.38 = f32[64]{0:T(128)S(1)} all-reduce(f32[64]{0:T(128)S(1)} %psum.37), channel_id=1, replica_groups=mesh['gx_0'=8,'gx_1'=2,'gx_2'=2,'gy_0'=2,'gy_1'=4] {'gy_0'}, use_global_device_ids=true, to_apply=%region_8.9 | all-reduce | flops 64 | bytes 512 | tf_op jit(solution)/shard_map/psum | solution.py:39
  272.0 6.0 %psum.39 = f32[64]{0:T(128)S(1)} all-reduce(f32[64]{0:T(128)S(1)} %psum.38), channel_id=1, replica_groups=mesh['gx_0'=8,'gx_1'=2,'gx_2'=2,'gy_0'=2,'gy_1'=4] {'gy_1'}, use_global_device_ids=true, to_apply=%region_9.10 | all-reduce | flops 64 | bytes 512 | tf_op jit(solution)/shard_map/psum | solution.py:39
  278.0 0.5 add_sqrt_fusion
  (73 shorter events, 5.0 us)
Async XLA Ops:
  8.3 20.3 %copy-start.1 = (s32[8,64,32]{1,2,0:T(8,128)S(1)}, s32[8,64,32]{1,2,0:T(8,128)}, u32[]{:S(2)}) copy-start(s32[8,64,32]{1,2,0:T(8,128)} %param.11) | copy-start | bytes 196612
  10.7 161.6 %collective-permute-start = (f32[1,64,2176]{2,1,0:T(8,128)}, f32[1,64,2176]{2,1,0:T(8,128)S(1)}, u32[]{:S(2)}, u32[]{:S(2)}) collective-permute-start(f32[1,64,2176]{2,1,0:T(8,128)} %get-tuple-element.72), channel_id=1, source_target_pairs={{0,8},{8,16},{16,24},{24,32},{32,40},{40,48},{48,56},{56,64},{64,7... | collective-permute-start | bytes 1671176 | tf_op jit(solution)/shard_map/ppermute | solution.py:30
  13.3 159.0 %collective-permute-start.1 = (f32[1,64,2176]{2,1,0:T(8,128)}, f32[1,64,2176]{2,1,0:T(8,128)S(1)}, u32[]{:S(2)}, u32[]{:S(2)}) collective-permute-start(f32[1,64,2176]{2,1,0:T(8,128)} %get-tuple-element.71), channel_id=1, source_target_pairs={{8,0},{16,8},{24,16},{32,24},{40,32},{48,40},{56,48},{64,56},{72,6... | collective-permute-start | bytes 1671176 | tf_op jit(solution)/shard_map/ppermute | solution.py:33
  15.2 132.4 %collective-permute-start.2 = (f32[8,1,2176]{2,0,1:T(8,128)S(1)}, f32[8,1,2176]{2,0,1:T(8,128)S(1)}, u32[]{:S(2)}, u32[]{:S(2)}) collective-permute-start(f32[8,1,2176]{2,0,1:T(8,128)S(1)} %copy.53), channel_id=1, source_target_pairs={{0,1},{1,2},{2,3},{3,4},{4,5},{5,6},{6,7},{8,9},{9,10},{10,11},{11... | collective-permute-start | bytes 208904 | tf_op jit(solution)/shard_map/ppermute | solution.py:30
  17.8 129.9 %collective-permute-start.3 = (f32[8,1,2176]{2,0,1:T(8,128)S(1)}, f32[8,1,2176]{2,0,1:T(8,128)}, u32[]{:S(2)}, u32[]{:S(2)}) collective-permute-start(f32[8,1,2176]{2,0,1:T(8,128)S(1)} %copy.55), channel_id=1, source_target_pairs={{1,0},{2,1},{3,2},{4,3},{5,4},{6,5},{7,6},{9,8},{10,9},{11,10},{12... | collective-permute-start | bytes 208904 | tf_op jit(solution)/shard_map/ppermute | solution.py:33
  119.9 13.0 %copy-start = (f32[8,64,32,64]{3,2,1,0:T(8,128)S(1)}, f32[8,64,32,64]{3,2,1,0:T(8,128)}, u32[]{:S(2)}) copy-start(f32[8,64,32,64]{3,2,1,0:T(8,128)} %get-tuple-element.151) | copy-start | bytes 12582916
  147.6 8.5 %slice-start = ((s8[4456448]{0:T(1024)(128)(4,1)}), s8[4194304]{0:T(1024)(128)(4,1)S(1)}, s32[]{:S(2)}) async-start(s8[4456448]{0:T(1024)(128)(4,1)} %bitcast.26), calls=%async_computation | async-start | bytes 8388608
  148.8 7.3 %slice-start.1 = ((s8[4456448]{0:T(1024)(128)(4,1)}), s8[262144]{0:T(1024)(128)(4,1)S(1)}, s32[]{:S(2)}) async-start(s8[4456448]{0:T(1024)(128)(4,1)} %bitcast.26), calls=%async_computation.1 | async-start | bytes 524288
  156.2 16.1 %slice-start.2 = ((s8[4456448]{0:T(1024)(128)(4,1)}), s8[262144]{0:T(1024)(128)(4,1)S(1)}, s32[]{:S(2)}) async-start(s8[4456448]{0:T(1024)(128)(4,1)} %bitcast.28), calls=%async_computation.2 | async-start | bytes 524288
  163.9 8.4 %slice-start.3 = ((s8[4456448]{0:T(1024)(128)(4,1)}), s8[4194304]{0:T(1024)(128)(4,1)S(1)}, s32[]{:S(2)}) async-start(s8[4456448]{0:T(1024)(128)(4,1)} %bitcast.28), calls=%async_computation.3 | async-start | bytes 8388608
where the time goes:
time: 283 us; the launch traced here: 278 us
  other arithmetic  96 us (34%)
  matrix products  65.3 us (23%)
  local copies, waits for them, and re-layouts  64.3 us (23%)
  blocking collectives  44.5 us (16%)
  starting transfers between devices  7.27 us (3%)
    psum x5, blocking collectives, over_axes(): return functools.reduce(lax.psum, axes, array)  44.5 us
    dot_general x8, matrix products, nonlinear_row(): jnp.dot(jnp.concatenate([current, charge], axis=0), analysis, precision=l...  34 us
    reduce_sum x1, other arithmetic, body(): partial_value = jnp.sum(residual * residual, axis=(0, 1, 2))  31.9 us
    dot_general x8, matrix products, nonlinear_row(): jnp.dot(flat, synthesis, precision=lax.Precision.HIGHEST, preferred_eleme...  31.4 us
    mul x2, other arithmetic, edge_flux(): return harmonic_mean(low_cond, high_cond) * (high_volt - low_volt)  17.1 us
    sub x2, local copies, waits for them, and re-layouts, edge_flux(): return harmonic_mean(low_cond, high_cond) * (high_volt - low_volt)  16.4 us
    mul x9, other arithmetic, time_derivative(): orders * coefs[..., half_count:]  13.9 us
    dynamic_update_slice x8, other arithmetic, body(): diode_part = lax.map(diode_rows, (volt_field, diode_field))  10.7 us
  transfers between devices with their start and end apart: 4, of which 0 were waited for; matrix products, arithmetic and copies ran while one was open for 55% of the time, Pallas kernels for 0%

commit v1 on v0

v1 whole, which is shorter than its diff:
```python
import functools
import math

import jax
import jax.numpy as jnp
import numpy as np
from jax import lax
from jax.experimental import pallas as pl
from jax.experimental.pallas import tpu as pltpu
from jax.sharding import PartitionSpec as P

NZ = 32
H = 32
KC = 64
S = 256
REGIONS = 8
BASE_FREQ = 0.1
NORM_EPS = 1e-06
LANES = 128
ZT = NZ * KC // LANES
PAD = 8
CHUNKS = 4

MESH = pl.DeviceIdType.MESH
F32 = jnp.float32
BF16 = jnp.bfloat16


def split(table):
    high = table.astype(jnp.bfloat16)
    low = (table - high.astype(np.float64)).astype(jnp.bfloat16)
    return high, low


def spectral_tables():
    orders = np.arange(1, H + 1, dtype=np.float64)
    steps = np.arange(S, dtype=np.int64)
    angles = 2.0 * math.pi * ((orders[:, None].astype(np.int64) * steps[None, :]) % S) / S
    cosines, sines = np.cos(angles), np.sin(angles)
    synthesis = np.concatenate([cosines, sines], axis=0)
    analysis = synthesis.T * (2.0 / S)
    freq = BASE_FREQ * orders
    derived = np.concatenate([freq * analysis[:, H:], -freq * analysis[:, :H]], axis=1)
    high, low = split(synthesis)
    ws = np.concatenate([high, high, low, low], axis=0)
    both = np.concatenate([analysis, derived], axis=0)
    high, low = split(both)
    wa = np.zeros((2, 2 * S, 2, LANES), jnp.bfloat16)
    for half in range(2):
        wa[half, :, 0, half * KC : half * KC + KC] = high
        wa[half, :, 1, half * KC : half * KC + KC] = low
    return ws, wa.reshape(4 * S, 2 * LANES)


def harmonic_mean(left, right):
    return 2.0 * left * right / (left + right)


def pick(region, table):
    value = jnp.full(region.shape, table[0], F32)
    for idx in range(1, REGIONS):
        value = jnp.where(region == idx, table[idx], value)
    return value


def widen(compact):
    rows, count = compact.shape
    return jnp.concatenate([compact, jnp.zeros((rows, LANES - count), compact.dtype)], axis=1)


def spread(compact, index):
    return jnp.take_along_axis(compact, index, axis=1, mode="promise_in_bounds")


def kernel(
    nx, ny, rows, cols, cells,
    volt, drive, region, mask, sigma, cap, ws_hbm, wa_hbm,
    out, norms,
    v, dr, reg, msk, con, ws, wa,
    halo_p, halo_n, reg_p, reg_n, col_l, col_r, reg_l, reg_r,
    x, s, y, nl, flux, par, ar_x, ar_y, mine,
    sem_v, sem_d, sem_s, send_h, recv_h, send_c, recv_c, send_y, recv_y, send_x, recv_x,
):
    gx, gy = lax.axis_index("gx"), lax.axis_index("gy")
    up, down = lax.rem(gx + 1, nx), lax.rem(gx + nx - 1, nx)
    right, left = lax.rem(gy + 1, ny), lax.rem(gy + ny - 1, ny)

    barrier = pltpu.get_barrier_semaphore()

    def greet_x(i, c):
        pl.semaphore_signal(barrier, inc=1, device_id={"gx": lax.rem(gx + i, nx)}, device_id_type=MESH)
        return c

    def greet_y(i, c):
        pl.semaphore_signal(barrier, inc=1, device_id={"gy": lax.rem(gy + i, ny)}, device_id_type=MESH)
        return c

    lax.fori_loop(1, nx, greet_x, 0)
    lax.fori_loop(1, ny, greet_y, 0)

    small = [
        pltpu.make_async_copy(region, reg, sem_s.at[0]),
        pltpu.make_async_copy(mask, msk, sem_s.at[1]),
        pltpu.make_async_copy(ws_hbm, ws, sem_s.at[2]),
        pltpu.make_async_copy(wa_hbm, wa, sem_s.at[3]),
    ]
    for copy in small:
        copy.start()

    def load_row(r, c):
        for zt in range(ZT):
            pltpu.make_async_copy(
                volt.at[r, :, pl.ds(zt * LANES, LANES)],
                v.at[r, zt, pl.ds(PAD, cols), :],
                sem_v.at[r],
            ).start()
        pltpu.make_async_copy(drive.at[r], dr.at[r], sem_d.at[r]).start()
        return c

    lax.fori_loop(0, rows, load_row, 0)

    pl.semaphore_wait(barrier, nx + ny - 2)
    sends = []

    def send(src, dst, ssem, rsem, where):
        copy = pltpu.make_async_remote_copy(
            src_ref=src, dst_ref=dst, send_sem=ssem, recv_sem=rsem,
            device_id=where, device_id_type=MESH,
        )
        copy.start()
        sends.append(copy)
        return copy

    to_right = [
        send(volt.at[:, pl.ds(cols - 1, 1), :], col_l, send_c.at[0], recv_c.at[0], {"gy": right}),
        send(region.at[:, pl.ds(cols - 8, 8), :], reg_l, send_c.at[1], recv_c.at[1], {"gy": right}),
    ]
    to_left = [
        send(volt.at[:, pl.ds(0, 1), :], col_r, send_c.at[2], recv_c.at[2], {"gy": left}),
        send(region.at[:, pl.ds(0, 8), :], reg_r, send_c.at[3], recv_c.at[3], {"gy": left}),
    ]
    reg_up = send(region.at[rows - 1], reg_p, send_h.at[0, CHUNKS], recv_h.at[0, CHUNKS], {"gx": up})
    reg_down = send(region.at[0], reg_n, send_h.at[1, CHUNKS], recv_h.at[1, CHUNKS], {"gx": down})
    piece = cols // CHUNKS
    ups, downs = [], []
    for k in range(CHUNKS):
        part = pl.ds(k * piece, piece)
        ups.append(send(volt.at[rows - 1, part, :], halo_p.at[part, :], send_h.at[0, k], recv_h.at[0, k], {"gx": up}))
        downs.append(send(volt.at[0, part, :], halo_n.at[part, :], send_h.at[1, k], recv_h.at[1, k], {"gx": down}))

    lane = lax.broadcasted_iota(jnp.int32, (8, LANES), 1)
    high = (lane >= KC).astype(jnp.int32)
    coef = lane % KC
    order = (coef % H + 1).astype(F32) * BASE_FREQ
    freq = jnp.where(coef < H, order, -order)
    partner = jnp.where(coef < H, lane + H, lane - H)
    own = [high + 2 * zt for zt in range(ZT)]
    within = [jnp.full((8, LANES), 2 * zt, jnp.int32) for zt in range(ZT)]
    across = [jnp.where(high == 0, 2 * zt - 1 if zt else NZ - 1, 2 * zt + 1) for zt in range(ZT)]
    left_half = lax.broadcasted_iota(jnp.int32, (cols, LANES), 1) < KC

    edge = jnp.zeros((PAD, LANES), F32)

    def clear(r, c):
        for zt in range(ZT):
            v[r, zt, pl.ds(0, PAD), :] = edge
            v[r, zt, pl.ds(cols + PAD, PAD), :] = edge
        return c

    lax.fori_loop(0, rows, clear, 0)
    flux[...] = jnp.zeros_like(flux)

    small[0].wait()

    def conduct_row(r, c):
        con[r] = pick(reg[r], sigma)
        return c

    lax.fori_loop(0, rows, conduct_row, 0)
    for copy in small[1:]:
        copy.wait()

    def wait_volt(r):
        whole = v.at[r, :, pl.ds(PAD, cols), :]
        pltpu.make_async_copy(whole, whole, sem_v.at[r]).wait()

    wait_volt(0)

    def one_row(r, c):
        after = jnp.minimum(r + 1, rows - 1)

        @pl.when(r < rows - 1)
        def _():
            wait_volt(r + 1)

        pltpu.make_async_copy(dr.at[r], dr.at[r], sem_d.at[r]).wait()

        here = widen(con[r])
        there = widen(con[after])
        live = jnp.where(r < rows - 1, 1.0, 0.0)
        col = lax.broadcasted_iota(jnp.int32, (cols, LANES), 0)
        z_lane = lax.broadcasted_iota(jnp.int32, (cols, LANES), 1)
        cell = z_lane < NZ
        par[0] = jnp.where(cell, harmonic_mean(here, there), 0.0) * live
        nxt = jnp.where(col == cols - 1, 0.0, pltpu.roll(here, cols - 1, 0))
        col_next = jnp.where(cell, harmonic_mean(here, nxt), 0.0)
        par[1] = col_next
        par[2] = jnp.where(col == 0, 0.0, pltpu.roll(col_next, 1, 0))
        deep = pltpu.roll(here, LANES - 1, 1)
        par[3] = jnp.where(z_lane < NZ - 1, harmonic_mean(here, deep), 0.0)
        par[4] = widen(pick(reg[r], cap))
        par[5] = widen(msk[r].astype(F32) * 0.5)

        for zt in range(ZT):
            value = v[r, zt, pl.ds(PAD, cols), :]
            near = value.astype(BF16).astype(F32)
            rest = value - near
            x[pl.ds(zt * cols, cols), :] = jnp.where(left_half, near, pltpu.roll(rest, KC, 1)).astype(BF16)
            x[pl.ds((ZT + zt) * cols, cols), :] = jnp.where(left_half, pltpu.roll(near, KC, 1), rest).astype(BF16)
        xs = x[...]
        s[...] = jnp.dot(jnp.concatenate([xs, xs], axis=1), ws[...], preferred_element_type=F32)
        for zt in range(ZT):
            for half in range(2):
                wave = s[pl.ds((half * ZT + zt) * cols, cols), :]
                bent = jnp.tanh(wave)
                soft = jnp.abs(wave) - jnp.log(1.0 + jnp.abs(bent))
                y[pl.ds(zt * cols, cols), pl.ds(half * 2 * S, S)] = soft.astype(BF16)
                y[pl.ds(zt * cols, cols), pl.ds(half * 2 * S + S, S)] = bent.astype(BF16)
        full = jnp.dot(y[...], wa[...], preferred_element_type=F32)
        nl[...] = full[:, :LANES] + full[:, LANES:]

        for j in range(cols // 8):
            g_row, g_next, g_prev, g_deep, capacity, diode = (par[i, pl.ds(8 * j, 8), :] for i in range(6))
            values = [v[r, zt, pl.ds(PAD + 8 * j, 8), :] for zt in range(ZT)]
            turned = [pltpu.roll(value, KC, 1) for value in values]
            for zt in range(ZT):
                value = values[zt]
                lanes = pl.ds(zt * LANES, LANES)
                spot = pl.ds(8 * j, 8)
                flow = spread(g_row, own[zt]) * (value - v[after, zt, pl.ds(PAD + 8 * j, 8), :])
                total = flow - flux[spot, lanes] - dr[r, spot, lanes]
                flux[spot, lanes] = flow
                total += spread(g_next, own[zt]) * (value - v[r, zt, pl.ds(PAD + 8 * j + 1, 8), :])
                total += spread(g_prev, own[zt]) * (value - v[r, zt, pl.ds(PAD + 8 * j - 1, 8), :])
                total += spread(g_deep, within[zt]) * (value - turned[zt])
                outer = jnp.where(high == 0, turned[max(zt - 1, 0)], turned[min(zt + 1, ZT - 1)])
                total += spread(g_deep, across[zt]) * (value - outer)
                total += spread(capacity, own[zt]) * (freq * spread(value, partner))
                total += spread(diode, own[zt]) * (value + nl[pl.ds(zt * cols + 8 * j, 8), :])
                out[r, spot, lanes] = total
        return c

    lax.fori_loop(0, rows, one_row, 0)

    for copy in to_right + to_left:
        copy.wait_recv()
    sub = lax.broadcasted_iota(jnp.int32, (8, LANES), 0)

    def fix_cols(r, acc):
        first = widen(con[r, pl.ds(0, 8), :])
        last = widen(con[r, pl.ds(cols - 8, 8), :])
        before = widen(pltpu.roll(pick(reg_l[r], sigma), 1, 0))
        behind = widen(pltpu.roll(pick(reg_r[r], sigma), 7, 0))
        g_l = jnp.where((sub == 0) & (lane < NZ) & (gy > 0), harmonic_mean(first, before), 0.0)
        g_r = jnp.where((sub == 7) & (lane < NZ) & (gy < ny - 1), harmonic_mean(last, behind), 0.0)
        for zt in range(ZT):
            lanes = pl.ds(zt * LANES, LANES)
            out[r, pl.ds(0, 8), lanes] += spread(g_l, own[zt]) * (
                v[r, zt, pl.ds(PAD, 8), :] - jnp.broadcast_to(col_l[r, :, lanes], (8, LANES))
            )
            out[r, pl.ds(cols - 8, 8), lanes] += spread(g_r, own[zt]) * (
                v[r, zt, pl.ds(PAD + cols - 8, 8), :] - jnp.broadcast_to(col_r[r, :, lanes], (8, LANES))
            )
        return acc

    lax.fori_loop(0, rows, fix_cols, 0)

    def squares(r, acc):
        parts = [jnp.zeros((8, LANES), F32) for _ in range(4)]
        for zt in range(ZT):
            for j in range(cols // 8):
                value = out[r, pl.ds(8 * j, 8), pl.ds(zt * LANES, LANES)]
                parts[j % 4] = parts[j % 4] + value * value
        return acc + ((parts[0] + parts[1]) + (parts[2] + parts[3]))

    acc = lax.fori_loop(1, rows - 1, squares, jnp.zeros((8, LANES), F32))

    for copies, notice, r, halo, marks in ((ups, reg_up, 0, halo_p, reg_p), (downs, reg_down, rows - 1, halo_n, reg_n)):
        notice.wait_recv()
        par[r // (rows - 1)] = jnp.where(
            lax.broadcasted_iota(jnp.int32, (cols, LANES), 1) < NZ,
            harmonic_mean(widen(con[r]), widen(pick(marks[...], sigma))),
            0.0,
        )
    for k in range(CHUNKS):
        for copies, r, halo in ((ups, 0, halo_p), (downs, rows - 1, halo_n)):
            copies[k].wait_recv()

            def fix_row(j, acc, r=r, halo=halo):
                base = pl.multiple_of(8 * j, 8)
                spot = pl.ds(base, 8)
                gain = par[r // (rows - 1), spot, :]
                parts = [jnp.zeros((8, LANES), F32) for _ in range(4)]
                for zt in range(ZT):
                    lanes = pl.ds(zt * LANES, LANES)
                    value = out[r, spot, lanes] + spread(gain, own[zt]) * (
                        v[r, zt, pl.ds(base + PAD, 8), :] - halo[spot, lanes]
                    )
                    out[r, spot, lanes] = value
                    parts[zt % 4] = parts[zt % 4] + value * value
                return acc + ((parts[0] + parts[1]) + (parts[2] + parts[3]))

            acc = lax.fori_loop(k * piece // 8, (k + 1) * piece // 8, fix_row, acc)

    local = jnp.sum(acc, axis=0, keepdims=True)
    mine[0] = local + pltpu.roll(local, KC, 1)

    def reduce_over(name, here, count, buf, slot, ssems, rsems):
        buf[here] = mine[slot]

        def copy_of(i):
            return pltpu.make_async_remote_copy(
                src_ref=mine.at[slot], dst_ref=buf.at[here], send_sem=ssems.at[i], recv_sem=rsems.at[i],
                device_id={name: lax.rem(here + i, count)}, device_id_type=MESH,
            )

        def begin(i, c):
            copy_of(i).start()
            return c

        def finish(i, c):
            copy_of(i).wait()
            return c

        lax.fori_loop(1, count, begin, 0)
        lax.fori_loop(1, count, finish, 0)
        total = buf[0]
        for i in range(1, count):
            total = total + buf[i]
        return total

    mine[1] = reduce_over("gy", gy, ny, ar_y, 0, send_y, recv_y)
    total = reduce_over("gx", gx, nx, ar_x, 1, send_x, recv_x)
    norms[...] = jnp.sqrt(total / cells + NORM_EPS)

    for copy in sends:
        copy.wait_send()


def body(nx, ny, volt, drive, region, diode_mask, sigma_table, cap_table):
    rows, cols, width = volt.shape
    cells = rows * cols * NZ * nx * ny
    ws, wa = spectral_tables()
    anywhere = pl.BlockSpec(memory_space=pl.ANY)
    smem = pl.BlockSpec(memory_space=pltpu.SMEM)
    vmem = pl.BlockSpec(memory_space=pltpu.VMEM)
    dma = pltpu.SemaphoreType.DMA
    residual, norms = pl.pallas_call(
        functools.partial(kernel, nx, ny, rows, cols, cells),
        out_shape=(
            jax.ShapeDtypeStruct((rows, cols, width), F32),
            jax.ShapeDtypeStruct((1, LANES), F32),
        ),
        in_specs=[anywhere] * 4 + [smem] * 2 + [anywhere] * 2,
        out_specs=(vmem, vmem),
        scratch_shapes=[
            pltpu.VMEM((rows, ZT, cols + 2 * PAD, LANES), F32),
            pltpu.VMEM((rows, cols, width), F32),
            pltpu.VMEM((rows, cols, NZ), jnp.int32),
            pltpu.VMEM((rows, cols, NZ), jnp.int32),
            pltpu.VMEM((rows, cols, NZ), F32),
            pltpu.VMEM(ws.shape, BF16),
            pltpu.VMEM(wa.shape, BF16),
            pltpu.VMEM((cols, width), F32),
            pltpu.VMEM((cols, width), F32),
            pltpu.VMEM((cols, NZ), jnp.int32),
            pltpu.VMEM((cols, NZ), jnp.int32),
            pltpu.VMEM((rows, 1, width), F32),
            pltpu.VMEM((rows, 1, width), F32),
            pltpu.VMEM((rows, 8, NZ), jnp.int32),
            pltpu.VMEM((rows, 8, NZ), jnp.int32),
            pltpu.VMEM((2 * ZT * cols, LANES), BF16),
            pltpu.VMEM((2 * ZT * cols, S), F32),
            pltpu.VMEM((ZT * cols, 4 * S), BF16),
            pltpu.VMEM((ZT * cols, LANES), F32),
            pltpu.VMEM((cols, width), F32),
            pltpu.VMEM((6, cols, LANES), F32),
            pltpu.VMEM((nx, 1, LANES), F32),
            pltpu.VMEM((ny, 1, LANES), F32),
            pltpu.VMEM((2, 1, LANES), F32),
            dma((rows,)), dma((rows,)), dma((4,)),
            dma((2, CHUNKS + 1)), dma((2, CHUNKS + 1)),
            dma((4,)), dma((4,)),
            dma((ny,)), dma((ny,)), dma((nx,)), dma((nx,)),
        ],
        compiler_params=pltpu.CompilerParams(
            collective_id=0, has_side_effects=True, vmem_limit_bytes=60 * 1024 * 1024
        ),
        name="residual",
    )(volt, drive, region, diode_mask, sigma_table, cap_table, ws, wa)
    return residual, norms[0, :KC]


def solution(mesh):
    nx, ny = mesh.shape["gx"], mesh.shape["gy"]
    cut = P("gx", "gy", None)
    return jax.shard_map(
        functools.partial(body, nx, ny), mesh=mesh, in_specs=(cut, cut, cut, cut, P(), P()),
        out_specs=(cut, P()), check_vma=False,
    )
```

time: 283 us -> 59.4 us (0.21); the launches traced: 278 us -> 59.2 us
  other arithmetic: 96 us -> 0 us
  matrix products: 65.3 us -> 0 us
  local copies, waits for them, and re-layouts: 64.3 us -> 9.36 us
  Pallas kernels: 0 us -> 49.2 us
  blocking collectives: 44.5 us -> 0 us
  starting transfers between devices: 7.27 us -> 0 us
    dot_general x16 -> x0, matrix products: 65.3 us -> none  [the longest x8 34 us: nonlinear_row(): jnp.dot(jnp.concatenate([current, charge], axis=0), analysis, precision=l...]
    pallas_call x0 -> x1, Pallas kernels: none -> 49.2 us  [body(): pl.pallas_call(functools.partial(kernel, nx, ny, rows, cols, cells), out_...]
    psum x5 -> x0, blocking collectives: 44.5 us -> none  [over_axes(): return functools.reduce(lax.psum, axes, array)]
    mul x23 -> x0, other arithmetic: 39.1 us -> none  [the longest x2 17.1 us: edge_flux(): return harmonic_mean(low_cond, high_cond) * (high_volt - low_volt)]
    reduce_sum x2 -> x0, other arithmetic: 33.6 us -> none  [the longest x1 31.9 us: body(): partial_value = jnp.sum(residual * residual, axis=(0, 1, 2))]
    reshape x3 -> x0, local copies, waits for them, and re-layouts: 23.4 us -> none  [the longest x1 7.81 us: body(): return (residual.reshape(rows_local, cols_local, row_width), norms_out)]
    sub x2 -> x0, local copies, waits for them, and re-layouts: 16.4 us -> none  [edge_flux(): return harmonic_mean(low_cond, high_cond) * (high_volt - low_volt)]
    dynamic_update_slice x8 -> x0, other arithmetic: 10.7 us -> none  [body(): diode_part = lax.map(diode_rows, (volt_field, diode_field))]
  transfers between devices with their start and end apart: 4 -> 0, of which waited for: 0 -> 0; matrix products, arithmetic and copies ran while one was open for 55% -> 0% of each run, Pallas kernels for 0% -> 0%
where the time goes in v1:
time: 59.4 us; the launch traced here: 59.2 us
  Pallas kernels  49.2 us (83%)
  local copies, waits for them, and re-layouts  9.36 us (16%)
  between operations  0.64 us (1%)
    pallas_call x1, Pallas kernels, body(): pl.pallas_call(functools.partial(kernel, nx, ny, rows, cols, cells), out_...  49.2 us
    unnamed x3, local copies, waits for them, and re-layouts  8.17 us
    squeeze x1, local copies, waits for them, and re-layouts, body(): return (residual, norms[0, :KC])  1.19 us

profile of v1, /device:TPU:1, one launch (start us, length us, event | category | flops | bytes accessed | tf_op | source)
XLA Modules:
  0.0 59.2 jit_solution(2329591835142335193)
XLA Ops:
  0.6 1.7 %copy.10.region = s32[8,64,32]{2,1,0:T(8,128)} copy(s32[8,64,32]{1,2,0:T(8,128)} %param.10) | data formatting | bytes 131072 | tf_op args[2]
  2.4 1.7 %copy.11.mask = s32[8,64,32]{2,1,0:T(8,128)} copy(s32[8,64,32]{1,2,0:T(8,128)} %param.11) | data formatting | bytes 131072 | tf_op args[3]
  4.1 49.2 %residual.1 = (f32[8,64,2048]{2,1,0:T(8,128)}, f32[1,128]{1,0:T(1,128)}) custom-call(f32[8,64,2048]{2,1,0:T(8,128)} %volt.1, f32[8,64,2048]{2,1,0:T(8,128)} %drive.1, s32[8,64,32]{2,1,0:T(8,128)} %copy.10.region, s32[8,64,32]{2,1,0:T(8,128)} %copy.11.mask, f32[8]{0:T(128)} %sigma.1, f32[8]{0:T(128)} %cap.1, bf16[256,256]{1,0:T(8,128)(2,1)} %constant.4.clone.ws_hbm, ...), custom_call_target="tpu_custom_call" | custom-call | tf_op jit(solution)/shard_map/residual/pallas_call | solution.py:358
  53.3 1.2 %slice_bitcast_fusion = f32[64]{0:T(128)} fusion(f32[1,128]{1,0:T(1,128)} %get-tuple-element.5), kind=kLoop, calls=%fused_computation | loop fusion | bytes 512 | tf_op jit(solution)/shard_map/squeeze | solution.py:401
  54.5 4.7 %copy.13 = f32[8,64,2048]{2,1,0:T(8,128)} copy(f32[8,64,2048]{2,1,0:T(8,128)} %get-tuple-element.8) | data formatting | bytes 8388608

commit v2 on v1

v2 whole, which is shorter than its diff:
```python
import functools
import math

import jax
import jax.numpy as jnp
import numpy as np
from jax import lax
from jax.experimental import pallas as pl
from jax.experimental.pallas import tpu as pltpu
from jax.sharding import PartitionSpec as P

NZ = 32
H = 32
KC = 64
S = 256
REGIONS = 8
BASE_FREQ = 0.1
NORM_EPS = 1e-06
LANES = 128
ZT = NZ * KC // LANES
PAD = 8
CHUNKS = 4
SEND_AT = 1

MESH = pl.DeviceIdType.MESH
F32 = jnp.float32
BF16 = jnp.bfloat16


def split(table):
    high = table.astype(jnp.bfloat16)
    low = (table - high.astype(np.float64)).astype(jnp.bfloat16)
    return high, low


def spectral_tables():
    orders = np.arange(1, H + 1, dtype=np.float64)
    steps = np.arange(S, dtype=np.int64)
    angles = 2.0 * math.pi * ((orders[:, None].astype(np.int64) * steps[None, :]) % S) / S
    cosines, sines = np.cos(angles), np.sin(angles)
    synthesis = np.concatenate([cosines, sines], axis=0)
    analysis = synthesis.T * (2.0 / S)
    freq = BASE_FREQ * orders
    derived = np.concatenate([freq * analysis[:, H:], -freq * analysis[:, :H]], axis=1)
    high, low = split(synthesis)
    ws = np.concatenate([high, high, low, low], axis=0)
    both = np.concatenate([analysis, derived], axis=0)
    high, low = split(both)
    wa = np.zeros((2, 2 * S, 2, LANES), jnp.bfloat16)
    for half in range(2):
        wa[half, :, 0, half * KC : half * KC + KC] = high
        wa[half, :, 1, half * KC : half * KC + KC] = low
    return ws, wa.reshape(4 * S, 2 * LANES)


def harmonic_mean(left, right):
    return 2.0 * left * right / (left + right)


def pick(region, table):
    value = jnp.full(region.shape, table[0], F32)
    for idx in range(1, REGIONS):
        value = jnp.where(region == idx, table[idx], value)
    return value


def widen(compact):
    rows, count = compact.shape
    return jnp.concatenate([compact, jnp.zeros((rows, LANES - count), compact.dtype)], axis=1)


def spread(compact, index):
    return jnp.take_along_axis(compact, index, axis=1, mode="promise_in_bounds")


def kernel(
    nx, ny, rows, cols, cells,
    volt, drive, region, mask, sigma, cap, ws_hbm, wa_hbm,
    out, norms,
    v, dr, reg, msk, ws, wa,
    halo_p, halo_n, reg_p, reg_n, col_l, col_r, con_l, con_r,
    x, s, y, nl, flux, turned, swapped, par, gain, ar_x, ar_y, mine,
    sem_v, sem_d, sem_s, send_h, recv_h, send_c, recv_c, send_y, recv_y, send_x, recv_x,
):
    gx, gy = lax.axis_index("gx"), lax.axis_index("gy")
    up, down = lax.rem(gx + 1, nx), lax.rem(gx + nx - 1, nx)
    right, left = lax.rem(gy + 1, ny), lax.rem(gy + ny - 1, ny)
    groups = cols // 8

    barrier = pltpu.get_barrier_semaphore()
    for i in range(1, nx):
        pl.semaphore_signal(barrier, inc=1, device_id={"gx": lax.rem(gx + i, nx)}, device_id_type=MESH)
    for i in range(1, ny):
        pl.semaphore_signal(barrier, inc=1, device_id={"gy": lax.rem(gy + i, ny)}, device_id_type=MESH)

    small = [
        pltpu.make_async_copy(region, reg, sem_s.at[0]),
        pltpu.make_async_copy(mask, msk, sem_s.at[1]),
        pltpu.make_async_copy(ws_hbm, ws, sem_s.at[2]),
        pltpu.make_async_copy(wa_hbm, wa, sem_s.at[3]),
    ]
    for copy in small:
        copy.start()

    def load_row(r, c):
        for zt in range(ZT):
            pltpu.make_async_copy(
                volt.at[r, :, pl.ds(zt * LANES, LANES)],
                v.at[r, zt, pl.ds(PAD, cols), :],
                sem_v.at[r],
            ).start()
        pltpu.make_async_copy(drive.at[r], dr.at[r], sem_d.at[r]).start()
        return c

    lax.fori_loop(0, rows, load_row, 0)

    def wait_volt(r):
        whole = v.at[r, :, pl.ds(PAD, cols), :]
        pltpu.make_async_copy(whole, whole, sem_v.at[r]).wait()

    def remote(src, dst, ssem, rsem, where):
        return pltpu.make_async_remote_copy(
            src_ref=src, dst_ref=dst, send_sem=ssem, recv_sem=rsem,
            device_id=where, device_id_type=MESH,
        )

    piece = cols // CHUNKS
    col_copies = [
        remote(volt.at[:, pl.ds(cols - 1, 1), :], col_l, send_c.at[0], recv_c.at[0], {"gy": right}),
        remote(par.at[:, 6, pl.ds(cols - 1, 1), :], con_l, send_c.at[1], recv_c.at[1], {"gy": right}),
        remote(volt.at[:, pl.ds(0, 1), :], col_r, send_c.at[2], recv_c.at[2], {"gy": left}),
        remote(par.at[:, 6, pl.ds(0, 1), :], con_r, send_c.at[3], recv_c.at[3], {"gy": left}),
    ]
    reg_copies = [
        remote(region.at[rows - 1], reg_p, send_h.at[0, CHUNKS], recv_h.at[0, CHUNKS], {"gx": up}),
        remote(region.at[0], reg_n, send_h.at[1, CHUNKS], recv_h.at[1, CHUNKS], {"gx": down}),
    ]
    row_copies = []
    for k in range(CHUNKS):
        part = pl.ds(k * piece, piece)
        row_copies.append((
            remote(volt.at[rows - 1, part, :], halo_p.at[part, :], send_h.at[0, k], recv_h.at[0, k], {"gx": up}),
            remote(volt.at[0, part, :], halo_n.at[part, :], send_h.at[1, k], recv_h.at[1, k], {"gx": down}),
        ))
    sends = reg_copies + col_copies + [copy for pair in row_copies for copy in pair]

    lane = lax.broadcasted_iota(jnp.int32, (8, LANES), 1)
    high = (lane >= KC).astype(jnp.int32)
    coef = lane % KC
    order = (coef % H + 1).astype(F32) * BASE_FREQ
    freq = jnp.where(coef < H, order, -order)
    partner = jnp.where(coef < H, lane + H, lane - H)
    own = [high + 2 * zt for zt in range(ZT)]
    within = [jnp.full((8, LANES), 2 * zt, jnp.int32) for zt in range(ZT)]
    across = [jnp.where(high == 0, 2 * zt - 1 if zt else NZ - 1, 2 * zt + 1) for zt in range(ZT)]
    left_half = lax.broadcasted_iota(jnp.int32, (cols, LANES), 1) < KC

    edge = jnp.zeros((PAD, LANES), F32)

    def clear(r, c):
        for zt in range(ZT):
            v[r, zt, pl.ds(0, PAD), :] = edge
            v[r, zt, pl.ds(cols + PAD, PAD), :] = edge
        return c

    lax.fori_loop(0, rows, clear, 0)
    flux[...] = jnp.zeros_like(flux)

    small[0].wait()
    small[1].wait()

    pairs = rows // 2
    pair_lane = lax.broadcasted_iota(jnp.int32, (NZ, LANES), 1)
    layer = lax.broadcasted_iota(jnp.int32, (NZ, LANES), 0)
    pair_regions = [jnp.concatenate([reg[2 * p], reg[2 * p + 1]], axis=1) for p in range(pairs)]
    conduct = [pick(both, sigma) for both in pair_regions]
    for p in range(pairs):
        here = conduct[p]
        beyond = pltpu.roll(conduct[p + 1], cols, 1) if p + 1 < pairs else jnp.zeros_like(here)
        there = jnp.where(pair_lane < cols, pltpu.roll(here, cols, 1), beyond)
        after = jnp.where(pair_lane % cols == cols - 1, 0.0, pltpu.roll(here, LANES - 1, 1))
        deeper = jnp.where(layer == NZ - 1, 0.0, pltpu.roll(here, NZ - 1, 0))
        g_next = harmonic_mean(here, after)
        diode = jnp.concatenate([msk[2 * p], msk[2 * p + 1]], axis=1).astype(F32) * 0.5
        fields = (
            harmonic_mean(here, there), g_next, pltpu.roll(g_next, 1, 1), harmonic_mean(here, deeper),
            pick(pair_regions[p], cap), diode, here,
        )
        for i, field in enumerate(fields):
            flat = widen(jnp.transpose(field))
            par[2 * p, i] = flat[:cols]
            par[2 * p + 1, i] = flat[cols:]
    for copy in small[2:]:
        copy.wait()
    wait_volt(0)

    def one_row(r, c):
        after = jnp.minimum(r + 1, rows - 1)

        @pl.when(r == SEND_AT)
        def _():
            pl.semaphore_wait(barrier, nx + ny - 2)
            for copy in sends:
                copy.start()

        @pl.when(r < rows - 1)
        def _():
            wait_volt(r + 1)

        pltpu.make_async_copy(dr.at[r], dr.at[r], sem_d.at[r]).wait()

        for zt in range(ZT):
            value = v[r, zt, pl.ds(PAD, cols), :]
            near = value.astype(BF16).astype(F32)
            rest = value - near
            x[pl.ds(zt * cols, cols), :] = jnp.where(left_half, near, pltpu.roll(rest, KC, 1)).astype(BF16)
            x[pl.ds((ZT + zt) * cols, cols), :] = jnp.where(left_half, pltpu.roll(near, KC, 1), rest).astype(BF16)
            turned[zt] = pltpu.roll(value, KC, 1)
            for j in range(groups):
                swapped[zt, pl.ds(8 * j, 8), :] = freq * spread(value[8 * j : 8 * j + 8], partner)
        xs = x[...]
        s[...] = jnp.dot(jnp.concatenate([xs, xs], axis=1), ws[...], preferred_element_type=F32)
        for zt in range(ZT):
            for half in range(2):
                wave = s[pl.ds((half * ZT + zt) * cols, cols), :]
                bent = jnp.tanh(wave)
                soft = jnp.abs(wave) - jnp.log(1.0 + jnp.abs(bent))
                y[pl.ds(zt * cols, cols), pl.ds(half * 2 * S, S)] = soft.astype(BF16)
                y[pl.ds(zt * cols, cols), pl.ds(half * 2 * S + S, S)] = bent.astype(BF16)
        full = jnp.dot(y[...], wa[...], preferred_element_type=F32)
        nl[...] = full[:, :LANES] + full[:, LANES:]

        for zt in range(ZT):
            lanes = pl.ds(zt * LANES, LANES)

            def gains(i, index):
                return [spread(par[r, i, pl.ds(8 * j, 8), :], index) for j in range(groups)]

            g_row, g_next, g_prev = gains(0, own[zt]), gains(1, own[zt]), gains(2, own[zt])
            capacity, diode = gains(4, own[zt]), gains(5, own[zt])
            g_in, g_out = gains(3, within[zt]), gains(3, across[zt])
            for j in range(groups):
                spot = pl.ds(8 * j, 8)
                value = v[r, zt, pl.ds(PAD + 8 * j, 8), :]
                flow = g_row[j] * (value - v[after, zt, pl.ds(PAD + 8 * j, 8), :])
                total = flow - flux[spot, lanes] - dr[r, spot, lanes]
                flux[spot, lanes] = flow
                total += g_next[j] * (value - v[r, zt, pl.ds(PAD + 8 * j + 1, 8), :])
                total += g_prev[j] * (value - v[r, zt, pl.ds(PAD + 8 * j - 1, 8), :])
                total += g_in[j] * (value - turned[zt, spot, :])
                outer = jnp.where(high == 0, turned[max(zt - 1, 0), spot, :], turned[min(zt + 1, ZT - 1), spot, :])
                total += g_out[j] * (value - outer)
                total += capacity[j] * swapped[zt, spot, :]
                total += diode[j] * (value + nl[pl.ds(zt * cols + 8 * j, 8), :])
                out[r, spot, lanes] = total
        return c

    lax.fori_loop(0, rows, one_row, 0)

    for copy in col_copies:
        copy.wait_recv()
    sub = lax.broadcasted_iota(jnp.int32, (8, LANES), 0)

    def fix_cols(r, c):
        first = par[r, 6, pl.ds(0, 8), :]
        last = par[r, 6, pl.ds(cols - 8, 8), :]
        before = jnp.broadcast_to(con_l[r], (8, LANES))
        behind = jnp.broadcast_to(con_r[r], (8, LANES))
        g_l = jnp.where((sub == 0) & (lane < NZ) & (gy > 0), harmonic_mean(first, before), 0.0)
        g_r = jnp.where((sub == 7) & (lane < NZ) & (gy < ny - 1), harmonic_mean(last, behind), 0.0)
        for zt in range(ZT):
            lanes = pl.ds(zt * LANES, LANES)
            out[r, pl.ds(0, 8), lanes] += spread(g_l, own[zt]) * (
                v[r, zt, pl.ds(PAD, 8), :] - jnp.broadcast_to(col_l[r, :, lanes], (8, LANES))
            )
            out[r, pl.ds(cols - 8, 8), lanes] += spread(g_r, own[zt]) * (
                v[r, zt, pl.ds(PAD + cols - 8, 8), :] - jnp.broadcast_to(col_r[r, :, lanes], (8, LANES))
            )
        return c

    lax.fori_loop(0, rows, fix_cols, 0)

    def squares(r, acc):
        parts = [jnp.zeros((8, LANES), F32) for _ in range(8)]
        for zt in range(ZT):
            for j in range(groups):
                value = out[r, pl.ds(8 * j, 8), pl.ds(zt * LANES, LANES)]
                parts[j % 8] = parts[j % 8] + value * value
        while len(parts) > 1:
            parts = [a + b for a, b in zip(parts[::2], parts[1::2])]
        return acc + parts[0]

    acc = lax.fori_loop(1, rows - 1, squares, jnp.zeros((8, LANES), F32))

    for end, (copy, marks, r) in enumerate(zip(reg_copies, (reg_p, reg_n), (0, rows - 1))):
        copy.wait_recv()
        field = jnp.concatenate([pick(marks[...], sigma), jnp.zeros((NZ, LANES - cols), F32)], axis=1)
        flat = widen(jnp.transpose(field))[:cols]
        inside = lax.broadcasted_iota(jnp.int32, (cols, LANES), 1) < NZ
        gain[end] = jnp.where(inside, harmonic_mean(par[r, 6], flat), 0.0)
    for k in range(CHUNKS):
        for end, (copy, halo, r) in enumerate(zip(row_copies[k], (halo_p, halo_n), (0, rows - 1))):
            copy.wait_recv()
            parts = [jnp.zeros((8, LANES), F32) for _ in range(8)]
            for j in range(k * piece // 8, (k + 1) * piece // 8):
                spot = pl.ds(8 * j, 8)
                for zt in range(ZT):
                    lanes = pl.ds(zt * LANES, LANES)
                    value = out[r, spot, lanes] + spread(gain[end, spot, :], own[zt]) * (
                        v[r, zt, pl.ds(8 * j + PAD, 8), :] - halo[spot, lanes]
                    )
                    out[r, spot, lanes] = value
                    parts[zt % 8] = parts[zt % 8] + value * value
            while len(parts) > 1:
                parts = [a + b for a, b in zip(parts[::2], parts[1::2])]
            acc = acc + parts[0]

    local = jnp.sum(acc, axis=0, keepdims=True)

    def reduce_over(name, here, count, value, buf, slot, ssem, rsem):
        mine[slot] = value
        buf[pl.ds(here, 1), :] = value
        for i in range(1, count):
            remote(mine.at[slot], buf.at[pl.ds(here, 1), :], ssem, rsem, {name: lax.rem(here + i, count)}).start()
        others = buf.at[pl.ds(0, count - 1), :]
        pltpu.make_async_copy(others, others, rsem).wait()
        return jnp.sum(buf[...], axis=0, keepdims=True)

    value = reduce_over("gy", gy, ny, local + pltpu.roll(local, KC, 1), ar_y, 0, send_y, recv_y)
    value = reduce_over("gx", gx, nx, value, ar_x, 1, send_x, recv_x)
    norms[...] = jnp.sqrt(value / cells + NORM_EPS)[0, :KC]

    for count, buf, ssem in ((ny, ar_y, send_y), (nx, ar_x, send_x)):
        others = buf.at[pl.ds(0, count - 1), :]
        pltpu.make_async_copy(others, others, ssem).wait()
    for copy in sends:
        copy.wait_send()


def body(nx, ny, volt, drive, region, diode_mask, sigma_table, cap_table):
    rows, cols, width = volt.shape
    cells = rows * cols * NZ * nx * ny
    ws, wa = spectral_tables()
    hbm = pl.BlockSpec(memory_space=pltpu.HBM)
    smem = pl.BlockSpec(memory_space=pltpu.SMEM)
    vmem = pl.BlockSpec(memory_space=pltpu.VMEM)
    dma = pltpu.SemaphoreType.DMA
    held = functools.partial(pltpu.with_memory_space_constraint, memory_space=pltpu.HBM)
    return pl.pallas_call(
        functools.partial(kernel, nx, ny, rows, cols, cells),
        out_shape=(
            jax.ShapeDtypeStruct((rows, cols, width), F32),
            jax.ShapeDtypeStruct((KC,), F32),
        ),
        in_specs=[hbm] * 4 + [smem] * 2 + [hbm] * 2,
        out_specs=(vmem, vmem),
        scratch_shapes=[
            pltpu.VMEM((rows, ZT, cols + 2 * PAD, LANES), F32),
            pltpu.VMEM((rows, cols, width), F32),
            pltpu.VMEM((rows, NZ, cols), jnp.int32),
            pltpu.VMEM((rows, NZ, cols), jnp.int32),
            pltpu.VMEM(ws.shape, BF16),
            pltpu.VMEM(wa.shape, BF16),
            pltpu.VMEM((cols, width), F32),
            pltpu.VMEM((cols, width), F32),
            pltpu.VMEM((NZ, cols), jnp.int32),
            pltpu.VMEM((NZ, cols), jnp.int32),
            pltpu.VMEM((rows, 1, width), F32),
            pltpu.VMEM((rows, 1, width), F32),
            pltpu.VMEM((rows, 1, LANES), F32),
            pltpu.VMEM((rows, 1, LANES), F32),
            pltpu.VMEM((2 * ZT * cols, LANES), BF16),
            pltpu.VMEM((2 * ZT * cols, S), F32),
            pltpu.VMEM((ZT * cols, 4 * S), BF16),
            pltpu.VMEM((ZT * cols, LANES), F32),
            pltpu.VMEM((cols, width), F32),
            pltpu.VMEM((ZT, cols, LANES), F32),
            pltpu.VMEM((ZT, cols, LANES), F32),
            pltpu.VMEM((rows, 7, cols, LANES), F32),
            pltpu.VMEM((2, cols, LANES), F32),
            pltpu.VMEM((nx, LANES), F32),
            pltpu.VMEM((ny, LANES), F32),
            pltpu.VMEM((2, 1, LANES), F32),
            dma((rows,)), dma((rows,)), dma((4,)),
            dma((2, CHUNKS + 1)), dma((2, CHUNKS + 1)),
            dma((4,)), dma((4,)),
            dma, dma, dma, dma,
        ],
        compiler_params=pltpu.CompilerParams(
            collective_id=0, has_side_effects=True, vmem_limit_bytes=38 * 1024 * 1024
        ),
        name="residual",
    )(
        held(volt), held(drive), held(jnp.swapaxes(region, 1, 2)), held(jnp.swapaxes(diode_mask, 1, 2)),
        sigma_table, cap_table, held(ws), held(wa),
    )


def solution(mesh):
    nx, ny = mesh.shape["gx"], mesh.shape["gy"]
    cut = P("gx", "gy", None)
    return jax.shard_map(
        functools.partial(body, nx, ny), mesh=mesh, in_specs=(cut, cut, cut, cut, P(), P()),
        out_specs=(cut, P()), check_vma=False,
    )
```

time: 59.4 us -> 45.2 us (0.76)
  Pallas kernels: 49.2 us -> 40.7 us
  local copies, waits for them, and re-layouts: 9.36 us -> 3.83 us
    pallas_call x1, Pallas kernels: 49.2 us -> 40.7 us  [body(): pl.pallas_call(functools.partial(kernel, nx, ny, rows, cols, cells), out_...]
    unnamed x3 -> x6, local copies, waits for them, and re-layouts: 8.17 us -> 3.83 us
    squeeze x1 -> x0, local copies, waits for them, and re-layouts: 1.19 us -> none  [body(): return (residual, norms[0, :KC])]
where the time goes in v2:
time: 45.2 us; the launch traced here: 45.1 us
  Pallas kernels  40.7 us (90%)
  local copies, waits for them, and re-layouts  3.83 us (8%)
  between operations  0.65 us (1%)
    pallas_call x1, Pallas kernels, body(): pl.pallas_call(functools.partial(kernel, nx, ny, rows, cols, cells), out_...  40.7 us
    unnamed x6, local copies, waits for them, and re-layouts  3.83 us

profile of v2, /device:TPU:1, one launch (start us, length us, event | category | flops | bytes accessed | tf_op | source)
XLA Modules:
  0.0 45.1 jit_solution(6248827715956962593)
XLA Ops:
  0.6 0.0 copy-start
  0.6 0.6 %copy-done = f32[8]{0:T(128)S(1)} copy-done((f32[8]{0:T(128)S(1)}, f32[8]{0:T(128)}, u32[]{:S(2)}) %copy-start) | copy-done | bytes 56
  1.3 0.0 copy-start.1
  1.3 0.7 %copy-done.1 = f32[8]{0:T(128)S(1)} copy-done((f32[8]{0:T(128)S(1)}, f32[8]{0:T(128)}, u32[]{:S(2)}) %copy-start.1) | copy-done | bytes 56
  1.9 40.7 %residual.1 = (f32[8,64,2048]{2,1,0:T(8,128)S(1)}, f32[64]{0:T(128)S(1)}) custom-call(f32[8,64,2048]{2,1,0:T(8,128)} %volt.1, f32[8,64,2048]{2,1,0:T(8,128)} %drive.1, s32[8,32,64]{2,1,0:T(8,128)} %bitcast.2, s32[8,32,64]{2,1,0:T(8,128)} %bitcast.3, f32[8]{0:T(128)S(1)} %copy-done, f32[8]{0:T(128)S(1)} %copy-done.1, bf16[256,256]{1,0:T(8,128)(2,1)} %constant.4.clone.ws_hbm, ...), custom_call_target="tpu_custom_call" | custom-call | tf_op jit(solution)/shard_map/residual/pallas_call | solution.py:349
  42.6 2.0 %copy.12 = f32[8,64,2048]{2,1,0:T(8,128)} copy(f32[8,64,2048]{2,1,0:T(8,128)S(1)} %get-tuple-element.4) | data formatting | bytes 8388608
  44.6 0.5 %copy.13 = f32[64]{0:T(128)} copy(f32[64]{0:T(128)S(1)} %get-tuple-element.5) | data formatting | bytes 512
Async XLA Ops:
  0.6 0.7 %copy-start = (f32[8]{0:T(128)S(1)}, f32[8]{0:T(128)}, u32[]{:S(2)}) copy-start(f32[8]{0:T(128)} %sigma.1) | copy-start | bytes 100
  1.3 0.7 %copy-start.1 = (f32[8]{0:T(128)S(1)}, f32[8]{0:T(128)}, u32[]{:S(2)}) copy-start(f32[8]{0:T(128)} %cap.1) | copy-start | bytes 100

commit v3 on v2

--- a/solution.py
+++ b/solution.py
@@ -18,6 +18,7 @@
 NORM_EPS = 1e-06
 LANES = 128
 ZT = NZ * KC // LANES
+INNER = 4
 PAD = 8
 CHUNKS = 4
 SEND_AT = 1
@@ -44,7 +45,7 @@
     derived = np.concatenate([freq * analysis[:, H:], -freq * analysis[:, :H]], axis=1)
     high, low = split(synthesis)
     ws = np.concatenate([high, high, low, low], axis=0)
-    both = np.concatenate([analysis, derived], axis=0)
+    both = 0.5 * np.concatenate([analysis, derived], axis=0)
     high, low = split(both)
     wa = np.zeros((2, 2 * S, 2, LANES), jnp.bfloat16)
     for half in range(2):
@@ -75,29 +76,25 @@
 
 def kernel(
     nx, ny, rows, cols, cells,
-    volt, drive, region, mask, sigma, cap, ws_hbm, wa_hbm,
+    volt, drive, region, mask, sigma_hbm, cap_hbm, ws_hbm, wa_hbm,
     out, norms,
-    v, dr, reg, msk, ws, wa,
+    sigma, cap, v, dr, reg, msk, ws, wa,
     halo_p, halo_n, reg_p, reg_n, col_l, col_r, con_l, con_r,
-    x, s, y, nl, flux, turned, swapped, par, gain, ar_x, ar_y, mine,
-    sem_v, sem_d, sem_s, send_h, recv_h, send_c, recv_c, send_y, recv_y, send_x, recv_x,
+    x, s, y, nl, flux, side, turned, par, gain, plane, line, mine,
+    sem_v, sem_d, sem_s, send_h, recv_h, send_c, recv_c, send_n, recv_n,
 ):
     gx, gy = lax.axis_index("gx"), lax.axis_index("gy")
     up, down = lax.rem(gx + 1, nx), lax.rem(gx + nx - 1, nx)
     right, left = lax.rem(gy + 1, ny), lax.rem(gy + ny - 1, ny)
     groups = cols // 8
 
-    barrier = pltpu.get_barrier_semaphore()
-    for i in range(1, nx):
-        pl.semaphore_signal(barrier, inc=1, device_id={"gx": lax.rem(gx + i, nx)}, device_id_type=MESH)
-    for i in range(1, ny):
-        pl.semaphore_signal(barrier, inc=1, device_id={"gy": lax.rem(gy + i, ny)}, device_id_type=MESH)
-
     small = [
         pltpu.make_async_copy(region, reg, sem_s.at[0]),
         pltpu.make_async_copy(mask, msk, sem_s.at[1]),
         pltpu.make_async_copy(ws_hbm, ws, sem_s.at[2]),
         pltpu.make_async_copy(wa_hbm, wa, sem_s.at[3]),
+        pltpu.make_async_copy(sigma_hbm, sigma, sem_s.at[4]),
+        pltpu.make_async_copy(cap_hbm, cap, sem_s.at[5]),
     ]
     for copy in small:
         copy.start()
@@ -114,6 +111,34 @@
 
     lax.fori_loop(0, rows, load_row, 0)
 
+    depth = nx // INNER
+    gz, gi = gx // INNER, lax.rem(gx, INNER)
+    base = gx - gi
+    near_i = [gi] + [lax.rem(gi + i, INNER) for i in range(1, INNER)]
+    near_y = [gy] + [lax.rem(gy + i, ny) for i in range(1, ny)]
+    in_plane = [
+        {"gx": base + near_i[i], "gy": near_y[k]} for k in range(ny) for i in range(INNER) if i or k
+    ]
+    in_line = [{"gx": lax.rem(gx + INNER * i, nx)} for i in range(1, depth)]
+
+    barrier = pltpu.get_barrier_semaphore()
+
+    def greet(where):
+        pl.semaphore_signal(barrier, inc=1, device_id=where, device_id_type=MESH)
+
+    for where in in_plane + in_line:
+        greet(where)
+
+    @pl.when(gi == INNER - 1)
+    def _():
+        greet({"gx": up})
+
+    @pl.when(gi == 0)
+    def _():
+        greet({"gx": down})
+
+    partners = len(in_plane) + len(in_line) + (gi == 0).astype(jnp.int32) + (gi == INNER - 1).astype(jnp.int32)
+
     def wait_volt(r):
         whole = v.at[r, :, pl.ds(PAD, cols), :]
         pltpu.make_async_copy(whole, whole, sem_v.at[r]).wait()
@@ -127,9 +152,9 @@
     piece = cols // CHUNKS
     col_copies = [
         remote(volt.at[:, pl.ds(cols - 1, 1), :], col_l, send_c.at[0], recv_c.at[0], {"gy": right}),
-        remote(par.at[:, 6, pl.ds(cols - 1, 1), :], con_l, send_c.at[1], recv_c.at[1], {"gy": right}),
+        remote(par.at[:, 4, pl.ds(cols - 1, 1), :], con_l, send_c.at[1], recv_c.at[1], {"gy": right}),
         remote(volt.at[:, pl.ds(0, 1), :], col_r, send_c.at[2], recv_c.at[2], {"gy": left}),
-        remote(par.at[:, 6, pl.ds(0, 1), :], con_r, send_c.at[3], recv_c.at[3], {"gy": left}),
+        remote(par.at[:, 4, pl.ds(0, 1), :], con_r, send_c.at[3], recv_c.at[3], {"gy": left}),
     ]
     reg_copies = [
         remote(region.at[rows - 1], reg_p, send_h.at[0, CHUNKS], recv_h.at[0, CHUNKS], {"gx": up}),
@@ -165,9 +190,11 @@
 
     lax.fori_loop(0, rows, clear, 0)
     flux[...] = jnp.zeros_like(flux)
-
-    small[0].wait()
-    small[1].wait()
+    for zt in range(ZT):
+        side[zt, pl.ds(0, PAD), :] = edge
+
+    for i in (0, 1, 4, 5):
+        small[i].wait()
 
     pairs = rows // 2
     pair_lane = lax.broadcasted_iota(jnp.int32, (NZ, LANES), 1)
@@ -180,26 +207,62 @@
         there = jnp.where(pair_lane < cols, pltpu.roll(here, cols, 1), beyond)
         after = jnp.where(pair_lane % cols == cols - 1, 0.0, pltpu.roll(here, LANES - 1, 1))
         deeper = jnp.where(layer == NZ - 1, 0.0, pltpu.roll(here, NZ - 1, 0))
-        g_next = harmonic_mean(here, after)
-        diode = jnp.concatenate([msk[2 * p], msk[2 * p + 1]], axis=1).astype(F32) * 0.5
+        diode = jnp.concatenate([msk[2 * p], msk[2 * p + 1]], axis=1)
+        held_charge = pick(pair_regions[p], cap)
         fields = (
-            harmonic_mean(here, there), g_next, pltpu.roll(g_next, 1, 1), harmonic_mean(here, deeper),
-            pick(pair_regions[p], cap), diode, here,
+            harmonic_mean(here, there), harmonic_mean(here, after), harmonic_mean(here, deeper),
+            jnp.where(diode != 0, -held_charge, held_charge), here,
         )
         for i, field in enumerate(fields):
             flat = widen(jnp.transpose(field))
             par[2 * p, i] = flat[:cols]
             par[2 * p + 1, i] = flat[cols:]
-    for copy in small[2:]:
-        copy.wait()
+    small[2].wait()
+    small[3].wait()
+
+    def pairs_of(r):
+        for zt in range(ZT):
+            value = v[r, zt, pl.ds(PAD, cols), :]
+            other = pltpu.roll(value, KC, 1)
+            rest = value - value.astype(BF16).astype(F32)
+            other_rest = other - other.astype(BF16).astype(F32)
+            x[pl.ds(zt * cols, cols), :] = jnp.where(left_half, value, other_rest).astype(BF16)
+            x[pl.ds((ZT + zt) * cols, cols), :] = jnp.where(left_half, other, rest).astype(BF16)
+            turned[zt] = other
+
+    def linear(r):
+        after = jnp.minimum(r + 1, rows - 1)
+        for zt in range(ZT):
+            lanes = pl.ds(zt * LANES, LANES)
+
+            def gains(i, index):
+                return [spread(par[r, i, pl.ds(8 * j, 8), :], index) for j in range(groups)]
+
+            g_row, g_next, charge = gains(0, own[zt]), gains(1, own[zt]), gains(3, own[zt])
+            g_in, g_out = gains(2, within[zt]), gains(2, across[zt])
+            for j in range(groups):
+                spot = pl.ds(8 * j, 8)
+                value = v[r, zt, pl.ds(PAD + 8 * j, 8), :]
+                flow = g_row[j] * (value - v[after, zt, pl.ds(PAD + 8 * j, 8), :])
+                total = flow - flux[spot, lanes] - dr[r, spot, lanes]
+                flux[spot, lanes] = flow
+                flow = g_next[j] * (value - v[r, zt, pl.ds(PAD + 8 * j + 1, 8), :])
+                side[zt, pl.ds(PAD + 8 * j, 8), :] = flow
+                total += flow - side[zt, pl.ds(PAD + 8 * j - 1, 8), :]
+                total += g_in[j] * (value - turned[zt, spot, :])
+                outer = jnp.where(high == 0, turned[max(zt - 1, 0), spot, :], turned[min(zt + 1, ZT - 1), spot, :])
+                total += g_out[j] * (value - outer)
+                total += jnp.abs(charge[j]) * (freq * spread(value, partner))
+                total += jnp.where(charge[j] < 0.0, 0.5 * value + nl[pl.ds(zt * cols + 8 * j, 8), :], 0.0)
+                out[r, spot, lanes] = total
+
     wait_volt(0)
+    pairs_of(0)
 
     def one_row(r, c):
-        after = jnp.minimum(r + 1, rows - 1)
-
         @pl.when(r == SEND_AT)
         def _():
-            pl.semaphore_wait(barrier, nx + ny - 2)
+            pl.semaphore_wait(barrier, partners)
             for copy in sends:
                 copy.start()
 
@@ -208,16 +271,6 @@
             wait_volt(r + 1)
 
         pltpu.make_async_copy(dr.at[r], dr.at[r], sem_d.at[r]).wait()
-
-        for zt in range(ZT):
-            value = v[r, zt, pl.ds(PAD, cols), :]
-            near = value.astype(BF16).astype(F32)
-            rest = value - near
-            x[pl.ds(zt * cols, cols), :] = jnp.where(left_half, near, pltpu.roll(rest, KC, 1)).astype(BF16)
-            x[pl.ds((ZT + zt) * cols, cols), :] = jnp.where(left_half, pltpu.roll(near, KC, 1), rest).astype(BF16)
-            turned[zt] = pltpu.roll(value, KC, 1)
-            for j in range(groups):
-                swapped[zt, pl.ds(8 * j, 8), :] = freq * spread(value[8 * j : 8 * j + 8], partner)
         xs = x[...]
         s[...] = jnp.dot(jnp.concatenate([xs, xs], axis=1), ws[...], preferred_element_type=F32)
         for zt in range(ZT):
@@ -229,30 +282,8 @@
                 y[pl.ds(zt * cols, cols), pl.ds(half * 2 * S + S, S)] = bent.astype(BF16)
         full = jnp.dot(y[...], wa[...], preferred_element_type=F32)
         nl[...] = full[:, :LANES] + full[:, LANES:]
-
-        for zt in range(ZT):
-            lanes = pl.ds(zt * LANES, LANES)
-
-            def gains(i, index):
-                return [spread(par[r, i, pl.ds(8 * j, 8), :], index) for j in range(groups)]
-
-            g_row, g_next, g_prev = gains(0, own[zt]), gains(1, own[zt]), gains(2, own[zt])
-            capacity, diode = gains(4, own[zt]), gains(5, own[zt])
-            g_in, g_out = gains(3, within[zt]), gains(3, across[zt])
-            for j in range(groups):
-                spot = pl.ds(8 * j, 8)
-                value = v[r, zt, pl.ds(PAD + 8 * j, 8), :]
-                flow = g_row[j] * (value - v[after, zt, pl.ds(PAD + 8 * j, 8), :])
-                total = flow - flux[spot, lanes] - dr[r, spot, lanes]
-                flux[spot, lanes] = flow
-                total += g_next[j] * (value - v[r, zt, pl.ds(PAD + 8 * j + 1, 8), :])
-                total += g_prev[j] * (value - v[r, zt, pl.ds(PAD + 8 * j - 1, 8), :])
-                total += g_in[j] * (value - turned[zt, spot, :])
-                outer = jnp.where(high == 0, turned[max(zt - 1, 0), spot, :], turned[min(zt + 1, ZT - 1), spot, :])
-                total += g_out[j] * (value - outer)
-                total += capacity[j] * swapped[zt, spot, :]
-                total += diode[j] * (value + nl[pl.ds(zt * cols + 8 * j, 8), :])
-                out[r, spot, lanes] = total
+        linear(r)
+        pairs_of(jnp.minimum(r + 1, rows - 1))
         return c
 
     lax.fori_loop(0, rows, one_row, 0)
@@ -261,9 +292,9 @@
         copy.wait_recv()
     sub = lax.broadcasted_iota(jnp.int32, (8, LANES), 0)
 
-    def fix_cols(r, c):
-        first = par[r, 6, pl.ds(0, 8), :]
-        last = par[r, 6, pl.ds(cols - 8, 8), :]
+    def fix_cols(r, acc):
+        first = par[r, 4, pl.ds(0, 8), :]
+        last = par[r, 4, pl.ds(cols - 8, 8), :]
         before = jnp.broadcast_to(con_l[r], (8, LANES))
         behind = jnp.broadcast_to(con_r[r], (8, LANES))
         g_l = jnp.where((sub == 0) & (lane < NZ) & (gy > 0), harmonic_mean(first, before), 0.0)
@@ -276,11 +307,7 @@
             out[r, pl.ds(cols - 8, 8), lanes] += spread(g_r, own[zt]) * (
                 v[r, zt, pl.ds(PAD + cols - 8, 8), :] - jnp.broadcast_to(col_r[r, :, lanes], (8, LANES))
             )
-        return c
-
-    lax.fori_loop(0, rows, fix_cols, 0)
-
-    def squares(r, acc):
+        inner = jnp.where((r > 0) & (r < rows - 1), 1.0, 0.0)
         parts = [jnp.zeros((8, LANES), F32) for _ in range(8)]
         for zt in range(ZT):
             for j in range(groups):
@@ -288,16 +315,16 @@
                 parts[j % 8] = parts[j % 8] + value * value
         while len(parts) > 1:
             parts = [a + b for a, b in zip(parts[::2], parts[1::2])]
-        return acc + parts[0]
-
-    acc = lax.fori_loop(1, rows - 1, squares, jnp.zeros((8, LANES), F32))
+        return acc + inner * parts[0]
+
+    acc = lax.fori_loop(0, rows, fix_cols, jnp.zeros((8, LANES), F32))
 
     for end, (copy, marks, r) in enumerate(zip(reg_copies, (reg_p, reg_n), (0, rows - 1))):
         copy.wait_recv()
         field = jnp.concatenate([pick(marks[...], sigma), jnp.zeros((NZ, LANES - cols), F32)], axis=1)
         flat = widen(jnp.transpose(field))[:cols]
         inside = lax.broadcasted_iota(jnp.int32, (cols, LANES), 1) < NZ
-        gain[end] = jnp.where(inside, harmonic_mean(par[r, 6], flat), 0.0)
+        gain[end] = jnp.where(inside, harmonic_mean(par[r, 4], flat), 0.0)
     for k in range(CHUNKS):
         for end, (copy, halo, r) in enumerate(zip(row_copies[k], (halo_p, halo_n), (0, rows - 1))):
             copy.wait_recv()
@@ -317,22 +344,24 @@
 
     local = jnp.sum(acc, axis=0, keepdims=True)
 
-    def reduce_over(name, here, count, value, buf, slot, ssem, rsem):
+    def reduce_over(others, here, value, buf, slot):
         mine[slot] = value
+        spot = buf.at[pl.ds(here, 1), :]
         buf[pl.ds(here, 1), :] = value
-        for i in range(1, count):
-            remote(mine.at[slot], buf.at[pl.ds(here, 1), :], ssem, rsem, {name: lax.rem(here + i, count)}).start()
-        others = buf.at[pl.ds(0, count - 1), :]
-        pltpu.make_async_copy(others, others, rsem).wait()
+        for where in others:
+            remote(mine.at[slot], spot, send_n.at[slot], recv_n.at[slot], where).start()
+        rest = buf.at[pl.ds(0, len(others)), :]
+        pltpu.make_async_copy(rest, rest, recv_n.at[slot]).wait()
         return jnp.sum(buf[...], axis=0, keepdims=True)
 
-    value = reduce_over("gy", gy, ny, local + pltpu.roll(local, KC, 1), ar_y, 0, send_y, recv_y)
-    value = reduce_over("gx", gx, nx, value, ar_x, 1, send_x, recv_x)
+    value = local + pltpu.roll(local, KC, 1)
+    value = reduce_over(in_plane, gy * INNER + gi, value, plane, 0)
+    value = reduce_over(in_line, gz, value, line, 1)
     norms[...] = jnp.sqrt(value / cells + NORM_EPS)[0, :KC]
 
-    for count, buf, ssem in ((ny, ar_y, send_y), (nx, ar_x, send_x)):
-        others = buf.at[pl.ds(0, count - 1), :]
-        pltpu.make_async_copy(others, others, ssem).wait()
+    for slot, buf in enumerate((plane, line)):
+        others = buf.at[pl.ds(0, buf.shape[0] - 1), :]
+        pltpu.make_async_copy(others, others, send_n.at[slot]).wait()
     for copy in sends:
         copy.wait_send()
 
@@ -342,7 +371,6 @@
     cells = rows * cols * NZ * nx * ny
     ws, wa = spectral_tables()
     hbm = pl.BlockSpec(memory_space=pltpu.HBM)
-    smem = pl.BlockSpec(memory_space=pltpu.SMEM)
     vmem = pl.BlockSpec(memory_space=pltpu.VMEM)
     dma = pltpu.SemaphoreType.DMA
     held = functools.partial(pltpu.with_memory_space_constraint, memory_space=pltpu.HBM)
@@ -352,9 +380,11 @@
             jax.ShapeDtypeStruct((rows, cols, width), F32),
             jax.ShapeDtypeStruct((KC,), F32),
         ),
-        in_specs=[hbm] * 4 + [smem] * 2 + [hbm] * 2,
+        in_specs=[hbm] * 8,
         out_specs=(vmem, vmem),
         scratch_shapes=[
+            pltpu.SMEM((REGIONS,), F32),
+            pltpu.SMEM((REGIONS,), F32),
             pltpu.VMEM((rows, ZT, cols + 2 * PAD, LANES), F32),
             pltpu.VMEM((rows, cols, width), F32),
             pltpu.VMEM((rows, NZ, cols), jnp.int32),
@@ -374,17 +404,17 @@
             pltpu.VMEM((ZT * cols, 4 * S), BF16),
             pltpu.VMEM((ZT * cols, LANES), F32),
             pltpu.VMEM((cols, width), F32),
+            pltpu.VMEM((ZT, cols + PAD, LANES), F32),
             pltpu.VMEM((ZT, cols, LANES), F32),
-            pltpu.VMEM((ZT, cols, LANES), F32),
-            pltpu.VMEM((rows, 7, cols, LANES), F32),
+            pltpu.VMEM((rows, 5, cols, LANES), F32),
             pltpu.VMEM((2, cols, LANES), F32),
-            pltpu.VMEM((nx, LANES), F32),
-            pltpu.VMEM((ny, LANES), F32),
+            pltpu.VMEM((ny * INNER, LANES), F32),
+            pltpu.VMEM((nx // INNER, LANES), F32),
             pltpu.VMEM((2, 1, LANES), F32),
-            dma((rows,)), dma((rows,)), dma((4,)),
+            dma((rows,)), dma((rows,)), dma((6,)),
             dma((2, CHUNKS + 1)), dma((2, CHUNKS + 1)),
             dma((4,)), dma((4,)),
-            dma, dma, dma, dma,
+            dma((2,)), dma((2,)),
         ],
         compiler_params=pltpu.CompilerParams(
             collective_id=0, has_side_effects=True, vmem_limit_bytes=38 * 1024 * 1024
@@ -392,7 +422,7 @@
         name="residual",
     )(
         held(volt), held(drive), held(jnp.swapaxes(region, 1, 2)), held(jnp.swapaxes(diode_mask, 1, 2)),
-        sigma_table, cap_table, held(ws), held(wa),
+        held(sigma_table), held(cap_table), held(ws), held(wa),
     )
 
 

time: 45.2 us -> 38.6 us (0.85)
  Pallas kernels: 40.7 us -> 35.3 us
  local copies, waits for them, and re-layouts: 3.83 us -> 2.53 us
    pallas_call x1, Pallas kernels: 40.7 us -> 35.3 us  [body(): pl.pallas_call(functools.partial(kernel, nx, ny, rows, cols, cells), out_...]
    unnamed x6 -> x2, local copies, waits for them, and re-layouts: 3.83 us -> 2.53 us
where the time goes in v3:
time: 38.6 us; the launch traced here: 38.5 us
  Pallas kernels  35.3 us (91%)
  local copies, waits for them, and re-layouts  2.53 us (7%)
  between operations  0.64 us (2%)
    pallas_call x1, Pallas kernels, body(): pl.pallas_call(functools.partial(kernel, nx, ny, rows, cols, cells), out_...  35.3 us
    unnamed x2, local copies, waits for them, and re-layouts  2.53 us

profile of v3, /device:TPU:1, one launch (start us, length us, event | category | flops | bytes accessed | tf_op | source)
XLA Modules:
  0.0 38.5 jit_solution(5420533706004562372)
XLA Ops:
  0.6 35.3 %residual.1 = (f32[8,64,2048]{2,1,0:T(8,128)S(1)}, f32[64]{0:T(128)S(1)}) custom-call(f32[8,64,2048]{2,1,0:T(8,128)} %volt.1, f32[8,64,2048]{2,1,0:T(8,128)} %drive.1, s32[8,32,64]{2,1,0:T(8,128)} %bitcast.2, s32[8,32,64]{2,1,0:T(8,128)} %bitcast.3, f32[8]{0:T(128)} %sigma_hbm.1, f32[8]{0:T(128)} %cap_hbm.1, bf16[256,256]{1,0:T(8,128)(2,1)} %constant.4.clone.ws_hbm, ...), custom_call_target="tpu_custom_call" | custom-call | tf_op jit(solution)/shard_map/residual/pallas_call | solution.py:377
  36.0 2.0 %copy.12 = f32[8,64,2048]{2,1,0:T(8,128)} copy(f32[8,64,2048]{2,1,0:T(8,128)S(1)} %get-tuple-element.4) | data formatting | bytes 8388608
  38.0 0.5 %copy.13 = f32[64]{0:T(128)} copy(f32[64]{0:T(128)S(1)} %get-tuple-element.5) | data formatting | bytes 512
